TPU v7x, 512 devices: a whole 4x4x16 slice. The times are simulated.
512 devices in a mesh: row: 16 (over y_hi, x, core), col: 32 (over z, y_lo).
Axes of the slice: x: 4, y: 4 (y_hi: 2, y_lo: 2; y = y_hi * 2 + y_lo), z: 16, core: 2. Of those that a mesh axis runs over, the one named last changes fastest.
Arguments:
- specimen: float32 [2, 2048, 8192], P(None, 'row', 'col'), may hold values from -6 to 6
- probe_field: float32 [2, 256, 256], replicated, may hold values from -6 to 6
- scan_offsets: int32 [16, 32, 2, 2], replicated, may hold values from -128 to 128, as said below
- live_counts: int32 [16, 32], replicated, may hold values from 1 to 2, as said below
- magnitudes: float32 [16, 32, 2, 256, 256], P('row', 'col'), may hold values from 0 to 2
Outputs:
- specimen_next: float32 [2, 2048, 8192], P(None, 'row', 'col')
- probe_next: float32 [2, 256, 256], replicated
Inputs may be any that keep to these rules, and one draw needn't show every extreme that they name: `scan_offsets`: rows of a patch start within -128 to 0 of the tile's first row, columns within -128 to 128 of its first column. Tile (a, b) owns the positions in its first live_counts[a, b] slots.
All inputs are finite; a program needn't handle non-finite values.
Results may differ from a plain program's by a relative error of at most 0.0003.
Values sent between devices are 32-bit elements; how exact they have to be, the bound alone decides.
A program may use at most 64 MiB of HBM per device.

v0:
```python
import math

import jax
import jax.numpy as jnp
from jax import lax
from jax.sharding import PartitionSpec as P

modulus_floor = 0.25
object_damping = 0.1
probe_damping = 0.1


def extended_2(block, sides, width):
    for axis, dim in sides:
        count = lax.axis_size(axis)
        forward = [(i, i + 1) for i in range(count - 1)]
        backward = [(target, source) for source, target in forward]
        low = lax.ppermute(
            lax.slice_in_dim(block, block.shape[dim] - width, None, axis=dim), axis, forward
        )
        high = lax.ppermute(lax.slice_in_dim(block, 0, width, axis=dim), axis, backward)
        block = jnp.concatenate([low, block, high], axis=dim)
    return block


def dft_tables(width):
    counter = jnp.arange(width, dtype=jnp.int32)
    phase = counter[:, None] * counter[None, :] % width
    angle = phase.astype(jnp.float32) * (2.0 * math.pi / width)
    factor = 1.0 / math.sqrt(width)
    return (jnp.cos(angle) * factor, jnp.sin(angle) * factor)


def matmul_right(left, table):
    return jnp.einsum("sjm,ml->sjl", left, table, precision=lax.Precision.HIGHEST)


def matmul_left(table, right):
    return jnp.einsum("kj,sjl->skl", table, right, precision=lax.Precision.HIGHEST)


def transform(wave_real, wave_imag, cosine, sine, direction):
    inner_real = matmul_right(wave_real, cosine) + direction * matmul_right(wave_imag, sine)
    inner_imag = matmul_right(wave_imag, cosine) - direction * matmul_right(wave_real, sine)
    outer_real = matmul_left(cosine, inner_real) + direction * matmul_left(sine, inner_imag)
    outer_imag = matmul_left(cosine, inner_imag) - direction * matmul_left(sine, inner_real)
    return (outer_real, outer_imag)


def fold_rims(wide, tile_r, tile_c, half):
    center = wide[:, 2 * half : 2 * half + tile_r, :]
    center = center.at[:, :half, :].add(wide[:, :half, :])
    center = center.at[:, tile_r - half :, :].add(wide[:, tile_r + 3 * half :, :])
    result = center[:, :, 2 * half : 2 * half + tile_c]
    result = result.at[:, :, :half].add(center[:, :, :half])
    result = result.at[:, :, tile_c - half :].add(center[:, :, tile_c + 3 * half :])
    return result


def shards(specimen, probe_field, scan_offsets, live_counts, magnitudes):
    width = probe_field.shape[1]
    half = width // 2
    tile_r = specimen.shape[1]
    tile_c = specimen.shape[2]
    slots = magnitudes.shape[2]
    row_place = lax.axis_index("row")
    col_place = lax.axis_index("col")
    zero_index = jnp.zeros((), jnp.int32)
    extended = extended_2(specimen, (("row", 1), ("col", 2)), half)
    offsets_here = scan_offsets[row_place, col_place]
    live = (jnp.arange(slots, dtype=jnp.int32) < live_counts[row_place, col_place]).astype(
        jnp.float32
    )[:, None, None]
    row_starts = offsets_here[:, 0] + half
    col_starts = offsets_here[:, 1] + half

    def extract(row_start, col_start):
        return lax.dynamic_slice(extended, (zero_index, row_start, col_start), (2, width, width))

    patches = jax.vmap(extract)(row_starts, col_starts)
    patch_real = patches[:, 0]
    patch_imag = patches[:, 1]
    probe_real = probe_field[0]
    probe_imag = probe_field[1]
    power = probe_real * probe_real + probe_imag * probe_imag
    cosine, sine = dft_tables(width)
    wave_real = probe_real * patch_real - probe_imag * patch_imag
    wave_imag = probe_real * patch_imag + probe_imag * patch_real
    far_real, far_imag = transform(wave_real, wave_imag, cosine, sine, 1.0)
    modulus = jnp.sqrt(far_real * far_real + far_imag * far_imag)
    factor = magnitudes[0, 0] / jnp.maximum(modulus, modulus_floor) - 1.0
    diff_real, diff_imag = transform(far_real * factor, far_imag * factor, cosine, sine, -1.0)
    diff_real = diff_real * live
    diff_imag = diff_imag * live
    grad_real = probe_real * diff_real + probe_imag * diff_imag
    grad_imag = probe_real * diff_imag - probe_imag * diff_real
    pieces = jnp.stack([grad_real, grad_imag, live * power], axis=1)
    layers = pieces.shape[1]

    def place(slot, total):
        start = (zero_index, row_starts[slot], col_starts[slot])
        current = lax.dynamic_slice(total, start, (layers, width, width))
        return lax.dynamic_update_slice(total, current + pieces[slot], start)

    start_total = jnp.zeros((layers, tile_r + 2 * half, tile_c + 2 * half), jnp.float32)
    buffer = lax.fori_loop(0, slots, place, start_total)
    wide = extended_2(buffer, (("row", 1), ("col", 2)), half)
    folded = fold_rims(wide, tile_r, tile_c, half)
    update = folded[:2]
    lighting = folded[2]
    damping = object_damping * jnp.max(power)
    specimen_next = specimen + update / (lighting + damping)
    local_terms = (
        jnp.sum(patch_real * diff_real + patch_imag * diff_imag, 0),
        jnp.sum(patch_real * diff_imag - patch_imag * diff_real, 0),
        jnp.sum(live * (patch_real * patch_real + patch_imag * patch_imag), 0),
    )
    sum_real, sum_imag, weight = lax.psum(
        (local_terms[0], local_terms[1], local_terms[2]), ("row", "col")
    )
    denominator = weight + probe_damping * jnp.mean(weight)
    probe_next = probe_field + jnp.stack([sum_real, sum_imag]) / denominator
    return (specimen_next, probe_next)


def solution(mesh):
    return jax.shard_map(
        shards,
        mesh=mesh,
        in_specs=(P(None, "row", "col"), P(), P(), P(), P("row", "col", None, None, None)),
        out_specs=(P(None, "row", "col"), P()),
        check_vma=False,
    )
```

profile of v0, /device:TPU:1, one launch (start us, length us, event | category | flops | bytes accessed | tf_op | source)
XLA Modules:
  0.0 656.2 jit_solution(3833202811847272772)
XLA Ops:
  7.2 4.6 collective-permute-start
  11.9 5.6 collective-permute-start.1
  17.4 1.1 slice_bitcast_fusion.1
  19.0 1.3 dynamic_slice.35
  20.3 1.0 fusion.148
  21.3 2.7 collective-permute-start.2
  24.0 1.3 collective-permute-start.3
  26.0 1.0 copy.32
  27.2 12.7 %collective-permute-done.2 = f32[2,384,128]{2,1,0:T(8,128)S(1)} collective-permute-done((f32[2,384,128]{2,1,0:T(8,128)}, f32[2,384,128]{2,1,0:T(8,128)S(1)}, u32[]{:S(2)}, u32[]{:S(2)}) %collective-permute-start.2) | collective-permute-done | bytes 393248 | tf_op jit(solution)/shard_map/ppermute | solution.py:18
  40.6 1.3 pad_maximum_fusion
  41.9 5.8 while.21
  42.5 2.3 bitcast_dynamic-update-slice_fusion.2
  45.4 2.2 bitcast_dynamic-update-slice_fusion.2
  47.7 2.9 fusion.49
  50.6 1.6 fusion.53
  52.2 1.6 convolution_subtract_fusion.1
  53.8 1.8 fusion.47
  55.6 1.6 convolution_add_fusion.1
  57.2 1.8 fusion.51
  59.0 2.0 fusion.8
  61.0 2.0 fusion.25
  63.0 1.6 fusion.41
  64.6 1.7 fusion.45
  66.3 1.7 fusion.5
  68.0 1.7 fusion.6
  69.7 1.6 fusion.43
  71.2 2.6 fusion.39
  73.9 2.4 fusion.4
  76.2 1.2 copy.44
  77.5 4.0 fusion.16
  81.4 1.3 pad_maximum_fusion.1
  83.0 38.2 %while.20 = (s32[]{:T(128)}, f32[3,384,512]{2,1,0:T(8,128)S(1)}, s32[2]{0:T(128)S(1)}, s32[2]{0:T(128)S(1)}, f32[2,3,256,256]{3,2,0,1:T(8,128)}, /*index=5*/s32[]{:T(128)}, s32[]{:T(128)}, s32[]{:T(128)}, s32[]{:T(128)}) while((s32[]{:T(128)}, f32[3,384,512]{2,1,0:T(8,128)S(1)}, s32[2]{0:T(128)S(1)}, s32[2]{0:T(128)S(1)}, ...), condition=%wide.region_1.2_spmd, body=%wide.region_0.1_spmd.sunk | while | flops 196616 | bytes 3932361 | solution.py:106
  88.1 1.4 bitcast_add_fusion.2
  89.5 11.6 %dynamic_update_slice.8 = f32[3,384,512]{2,1,0:T(8,128)S(1)} dynamic-update-slice(f32[3,384,512]{2,1,0:T(8,128)S(1)} %get-tuple-element.311, f32[3,256,256]{2,1,0:T(8,128)S(1)} %bitcast_add_fusion.2, s32[]{:T(128)} %constant.194.clone.1..sunk, s32[]{:T(128)S(6)} %select_n.146, s32[]{:T(128)S(6)} %select_n.147) | dynamic-update-slice | bytes 1572868 | tf_op jit(solution)/shard_map/while/body/eval_jaxpr/dynamic_update_slice | solution.py:103
  106.3 1.4 bitcast_add_fusion.2
  107.7 13.5 %dynamic_update_slice.8 = f32[3,384,512]{2,1,0:T(8,128)S(1)} dynamic-update-slice(f32[3,384,512]{2,1,0:T(8,128)S(1)} %get-tuple-element.311, f32[3,256,256]{2,1,0:T(8,128)S(1)} %bitcast_add_fusion.2, s32[]{:T(128)} %constant.194.clone.1..sunk, s32[]{:T(128)S(6)} %select_n.146, s32[]{:T(128)S(6)} %select_n.147) | dynamic-update-slice | bytes 1572868 | tf_op jit(solution)/shard_map/while/body/eval_jaxpr/dynamic_update_slice | solution.py:103
  121.4 2.5 collective-permute-start.4
  123.8 1.9 collective-permute-start.5
  125.8 7.0 %collective-permute-done.4 = f32[3,128,512]{2,1,0:T(8,128)S(1)} collective-permute-done((f32[3,128,512]{2,1,0:T(8,128)S(1)}, f32[3,128,512]{2,1,0:T(8,128)S(1)}, u32[]{:S(2)}, u32[]{:S(2)}) %collective-permute-start.4) | collective-permute-done | bytes 786464 | tf_op jit(solution)/shard_map/ppermute | solution.py:18
  133.0 4.1 collective-permute-done.5
  137.2 1.1 fusion.146
  138.3 1.1 copy-done.1
  139.4 3.7 collective-permute-start.6
  143.1 1.3 collective-permute-start.7
  145.8 493.7 %all-reduce.3.cloned.1.call-done = (f32[1,256,256]{2,1,0:T(8,128)}, f32[1,256,256]{2,1,0:T(8,128)}, f32[256,256]{1,0:T(8,128)}) async-done(((f32[1,256,256]{2,1,0:T(8,128)}, f32[1,256,256]{2,1,0:T(8,128)}, f32[256,256]{1,0:T(8,128)}), (f32[1,256,256]{2,1,0:T(8,128)}, f32[1,256,256]{2,1,0:T(8,128)}, f32[256,256]{1,0:T(8,128)})) %all-reduce.3.cloned.1.call-update) | async-done | bytes 786448 | tf_op jit(solution)/shard_map/psum | solution.py:118
  639.5 1.6 reduce_sum.39
  642.8 1.9 fusion.10
  644.7 1.9 fusion.9
  (56 shorter events, 11.2 us)
Async XLA Ops:
  7.2 11.4 %copy-start = (s32[16,32,2,2]{1,3,2,0:T(2,128)S(1)}, s32[16,32,2,2]{1,3,2,0:T(2,128)}, u32[]{:S(2)}) copy-start(s32[16,32,2,2]{1,3,2,0:T(2,128)} %param.21) | copy-start | bytes 24580
  7.2 13.1 %copy-start.5 = (f32[2,128,256]{2,1,0:T(8,128)S(1)}, f32[2,128,256]{2,1,0:T(8,128)}, u32[]{:S(2)}) copy-start(f32[2,128,256]{2,1,0:T(8,128)} %param.19) | copy-start | bytes 786436
  7.2 632.3 %all-reduce.3.cloned.1.call-start = ((), (), s32[]{:S(2)}) async-start(), calls=%async_computation | async-start | bytes 1572864 | tf_op jit(solution)/shard_map/psum | solution.py:118
  7.2 13.0 %collective-permute-start = (f32[2,128,256]{2,1,0:T(8,128)}, f32[2,128,256]{2,1,0:T(8,128)S(1)}, u32[]{:S(2)}, u32[]{:S(2)}) collective-permute-start(f32[2,128,256]{2,1,0:T(8,128)} %param.19), channel_id=1, source_target_pairs={{0,32},{32,64},{64,96},{96,128},{128,160},{160,192},{192,224},{224... | collective-permute-start | bytes 786440 | tf_op jit(solution)/shard_map/ppermute | solution.py:18
  11.9 8.4 %collective-permute-start.1 = (f32[2,128,256]{2,1,0:T(8,128)}, f32[2,128,256]{2,1,0:T(8,128)S(1)}, u32[]{:S(2)}, u32[]{:S(2)}) collective-permute-start(f32[2,128,256]{2,1,0:T(8,128)} %param.19), channel_id=1, source_target_pairs={{32,0},{64,32},{96,64},{128,96},{160,128},{192,160},{224,192},{256... | collective-permute-start | bytes 786440 | tf_op jit(solution)/shard_map/ppermute | solution.py:21
  20.2 5.7 copy-start.7
  21.3 18.5 %collective-permute-start.2 = (f32[2,384,128]{2,1,0:T(8,128)}, f32[2,384,128]{2,1,0:T(8,128)S(1)}, u32[]{:S(2)}, u32[]{:S(2)}) collective-permute-start(f32[2,384,128]{2,1,0:T(8,128)} %get-tuple-element.217), channel_id=1, source_target_pairs={{0,1},{1,2},{2,3},{3,4},{4,5},{5,6},{6,7},{7,8},{8,9},{9,10},{10,1... | collective-permute-start | bytes 1179656 | tf_op jit(solution)/shard_map/ppermute | solution.py:18
  24.0 16.6 %collective-permute-start.3 = (f32[2,384,128]{2,1,0:T(8,128)}, f32[2,384,128]{2,1,0:T(8,128)}, u32[]{:S(2)}, u32[]{:S(2)}) collective-permute-start(f32[2,384,128]{2,1,0:T(8,128)} %get-tuple-element.218), channel_id=1, source_target_pairs={{1,0},{2,1},{3,2},{4,3},{5,4},{6,5},{7,6},{8,7},{9,8},{10,9},{11,1... | collective-permute-start | bytes 1179656 | tf_op jit(solution)/shard_map/ppermute | solution.py:21
  39.8 0.8 copy-start.9
  47.7 2.9 copy-start.4
  57.2 3.8 copy-start.8
  121.4 11.4 %collective-permute-start.4 = (f32[3,128,512]{2,1,0:T(8,128)S(1)}, f32[3,128,512]{2,1,0:T(8,128)S(1)}, u32[]{:S(2)}, u32[]{:S(2)}) collective-permute-start(f32[3,128,512]{2,1,0:T(8,128)S(1)} %get-tuple-element.210), channel_id=1, source_target_pairs={{0,32},{32,64},{64,96},{96,128},{128,160},{160,192},{192,224},{224... | collective-permute-start | bytes 2359304 | tf_op jit(solution)/shard_map/ppermute | solution.py:18
  123.8 13.3 %collective-permute-start.5 = (f32[3,128,512]{2,1,0:T(8,128)S(1)}, f32[3,128,512]{2,1,0:T(8,128)S(1)}, u32[]{:S(2)}, u32[]{:S(2)}) collective-permute-start(f32[3,128,512]{2,1,0:T(8,128)S(1)} %get-tuple-element.209), channel_id=1, source_target_pairs={{32,0},{64,32},{96,64},{128,96},{160,128},{192,160},{224,192},{256... | collective-permute-start | bytes 2359304 | tf_op jit(solution)/shard_map/ppermute | solution.py:21
  137.2 2.2 copy-start.1
  137.2 7.2 %copy-start.3 = (f32[2,256,256]{2,1,0:T(8,128)S(1)}, f32[2,256,256]{2,1,0:T(8,128)}, u32[]{:S(2)}) copy-start(f32[2,256,256]{2,1,0:T(8,128)} %param.20) | copy-start | bytes 1572868
  139.4 505.3 %collective-permute-start.6 = (f32[3,640,128]{2,1,0:T(8,128)}, f32[3,640,128]{2,1,0:T(8,128)S(1)}, u32[]{:S(2)}, u32[]{:S(2)}) collective-permute-start(f32[3,640,128]{2,1,0:T(8,128)} %get-tuple-element.207), channel_id=1, source_target_pairs={{0,1},{1,2},{2,3},{3,4},{4,5},{5,6},{6,7},{7,8},{8,9},{9,10},{10,1... | collective-permute-start | bytes 2949128 | tf_op jit(solution)/shard_map/ppermute | solution.py:18
  143.1 501.6 %collective-permute-start.7 = (f32[3,640,128]{2,1,0:T(8,128)S(1)}, f32[3,640,128]{2,1,0:T(8,128)S(1)}, u32[]{:S(2)}, u32[]{:S(2)}) collective-permute-start(f32[3,640,128]{2,1,0:T(8,128)S(1)} %get-tuple-element.208), channel_id=1, source_target_pairs={{1,0},{2,1},{3,2},{4,3},{5,4},{6,5},{7,6},{8,7},{9,8},{10,9},{11,1... | collective-permute-start | bytes 2949128 | tf_op jit(solution)/shard_map/ppermute | solution.py:21
  644.7 2.8 copy-start.2
  647.6 1.0 copy-start.6
Sparse Core Ops, SparseCore 0:
  144.5 494.9 all-reduce.2
where the time goes:
time: 656 us
  waiting for transfers between devices  517 us (79%)
  local copies, waits for them, and re-layouts  43.7 us (7%)
  matrix products  32.4 us (5%)
  starting transfers between devices  23.5 us (4%)
  between operations  15.8 us (2%)
  other arithmetic  15.6 us (2%)
  loops' own time  7.67 us (1%)
    psum x1, waiting for transfers between devices, shards(): lax.psum((local_terms[0], local_terms[1], local_terms[2]), ('row', 'col'))  494 us
    dynamic_update_slice x2, local copies, waits for them, and re-layouts, place(): return lax.dynamic_update_slice(total, current + pieces[slot], start)  25.1 us
    ppermute x4, waiting for transfers between devices, extended_2(): lax.ppermute(lax.slice_in_dim(block, block.shape[dim] - width, None, axis...  19.6 us
    dot_general x8, matrix products, matmul_left(): jnp.einsum('kj,sjl->skl', table, right, precision=lax.Precision.HIGHEST)  18.1 us
    dot_general x8, matrix products, matmul_right(): jnp.einsum('sjm,ml->sjl', left, table, precision=lax.Precision.HIGHEST)  14.3 us
    ppermute x4, starting transfers between devices, extended_2(): lax.ppermute(lax.slice_in_dim(block, block.shape[dim] - width, None, axis...  13.4 us
  transfers between devices with their start and end apart: 9, of which 4 were waited for; matrix products, arithmetic and copies ran while one was open for 2% of the time, Pallas kernels for 0%

commit v1 on v0

--- a/solution.py
+++ b/solution.py
@@ -3,11 +3,247 @@
 import jax
 import jax.numpy as jnp
 from jax import lax
+from jax.experimental import pallas as pl
+from jax.experimental.pallas import tpu as pltpu
 from jax.sharding import PartitionSpec as P
 
 modulus_floor = 0.25
 object_damping = 0.1
 probe_damping = 0.1
+
+
+MESH = pl.DeviceIdType.MESH
+PEERS = 22
+
+
+def reduce_kernel(d_ref, probe_ref, out_ref, rp, s0, r1, s1, r2, s2, r3, g, wp, rw, r3w, ps, pr, ss, rs, ws, wr, zs, zr, gs, gr):
+    row = lax.axis_index("row")
+    col = lax.axis_index("col")
+    core = row % 2
+    x = (row // 2) % 4
+    y = (row // 8) * 2 + col % 2
+    z = col // 2
+
+    def device(core_of, x_of, y_of, z_of):
+        return ((y_of // 2) * 8 + x_of * 2 + core_of, z_of * 2 + y_of % 2)
+
+    def copy(src, dst, send, recv, where):
+        return pltpu.make_async_remote_copy(src_ref=src, dst_ref=dst, send_sem=send, recv_sem=recv, device_id=where, device_id_type=MESH)
+
+    partner = device(1 - core, x, y, z)
+    along = (
+        [device(core, (x + d) % 4, y, z) for d in range(1, 4)],
+        [device(core, x, (y + d) % 4, z) for d in range(1, 4)],
+    )
+    place = (x, y)
+
+    barrier = pltpu.get_barrier_semaphore()
+    pl.semaphore_signal(barrier, inc=1, device_id=partner, device_id_type=MESH)
+    for group in along:
+        for peer in group:
+            pl.semaphore_signal(barrier, inc=1, device_id=peer, device_id_type=MESH)
+
+    def greet(i, carry):
+        pl.semaphore_signal(barrier, inc=1, device_id=device(core, x, y, (z + i) % 16), device_id_type=MESH)
+        return carry
+
+    lax.fori_loop(1, 16, greet, 0)
+    total = d_ref[0, 2]
+    for t in range(1, 64):
+        total = total + d_ref[t, 2]
+    wp[0] = total
+    pl.semaphore_wait(barrier, PEERS)
+
+    pending = []
+    c = copy(d_ref.at[pl.ds((1 - core) * 32, 32)], rp, ps.at[0], pr.at[0], partner)
+    c.start()
+    cw = copy(wp.at[0], rw.at[0], ps.at[1], pr.at[1], partner)
+    cw.start()
+    pending += [c, cw]
+    c.wait_recv()
+    cw.wait_recv()
+    base = core * 32
+
+    def join(t, carry):
+        s0[t] = d_ref[base + t] + rp[t]
+        return carry
+
+    lax.fori_loop(0, 32, join, 0, unroll=4)
+    wp[1] = wp[0] + rw[0]
+
+    stage = []
+    for color in range(2):
+        for d in range(1, 4):
+            to = (place[color] + d) % 4
+            c = copy(s0.at[pl.ds(color * 16 + to * 4, 4)], r1.at[color, d - 1], ss.at[0, color, d - 1], rs.at[0, color, d - 1], along[color][d - 1])
+            c.start()
+            stage.append(c)
+    for d in range(1, 4):
+        c = copy(wp.at[1], rw.at[d], ws.at[0, d - 1], wr.at[0, d - 1], along[0][d - 1])
+        c.start()
+        stage.append(c)
+    for c in stage:
+        c.wait_recv()
+    pending += stage
+    for color in range(2):
+        for b in range(4):
+            s1[color, b] = s0[color * 16 + place[color] * 4 + b] + (r1[color, 0, b] + (r1[color, 1, b] + r1[color, 2, b]))
+    wp[2] = wp[1] + (rw[1] + (rw[2] + rw[3]))
+
+    stage = []
+    for color in range(2):
+        other = 1 - color
+        for d in range(1, 4):
+            to = (place[other] + d) % 4
+            c = copy(s1.at[color, to], r2.at[color, d - 1], ss.at[1, color, d - 1], rs.at[1, color, d - 1], along[other][d - 1])
+            c.start()
+            stage.append(c)
+    for d in range(1, 4):
+        c = copy(wp.at[2], rw.at[3 + d], ws.at[1, d - 1], wr.at[1, d - 1], along[1][d - 1])
+        c.start()
+        stage.append(c)
+    for c in stage:
+        c.wait_recv()
+    pending += stage
+    for color in range(2):
+        s2[color] = s1[color, place[1 - color]] + (r2[color, 0] + (r2[color, 1] + r2[color, 2]))
+    wp[3] = wp[2] + (rw[4] + (rw[5] + rw[6]))
+
+    def root(color):
+        return 2 + 8 * color + 4 * core
+
+    def slot(color):
+        return core * 32 + color * 16 + place[color] * 4 + place[1 - color]
+
+    for color in range(2):
+        goal = root(color)
+
+        @pl.when(z != goal)
+        def _():
+            at = (z - goal + 16) % 16
+            copy(s2.at[color], r3.at[at - 1], zs.at[color, 0], zr.at[0], device(core, x, y, goal)).start()
+            copy(wp.at[3], r3w.at[at - 1], zs.at[color, 1], zr.at[1], device(core, x, y, goal)).start()
+
+    for color in range(2):
+
+        @pl.when(z == root(color))
+        def _():
+            pltpu.make_async_copy(r3, r3, zr.at[0]).wait()
+            pltpu.make_async_copy(r3w, r3w, zr.at[1]).wait()
+            full = s2[color]
+            weight = wp[3]
+            for i in range(15):
+                full = full + r3[i]
+                weight = weight + r3w[i]
+            mean = jnp.sum(weight) * (1.0 / 65536.0)
+            scale = full[2] + 0.1 * mean
+            t = slot(color)
+            g[t, 0] = probe_ref[t, 0] + full[0] / scale
+            g[t, 1] = probe_ref[t, 1] + full[1] / scale
+
+            def send(i, carry):
+                copy(g.at[t], g.at[t], gs.at[i - 1], gr.at[color], device(core, x, y, (z + i) % 16)).start()
+                return carry
+
+            lax.fori_loop(1, 16, send, 0)
+
+    for color in range(2):
+
+        @pl.when(z != root(color))
+        def _():
+            t = slot(color)
+            pltpu.make_async_copy(g.at[t], g.at[t], gr.at[color]).wait()
+
+    stage = []
+    for color in range(2):
+        other = 1 - color
+        t = slot(color)
+        for d in range(1, 4):
+            c = copy(g.at[t], g.at[t], ss.at[2, color, d - 1], rs.at[2, color, d - 1], along[other][d - 1])
+            c.start()
+            stage.append(c)
+    for c in stage:
+        c.wait_recv()
+    pending += stage
+    stage = []
+    for color in range(2):
+        t = core * 32 + color * 16 + place[color] * 4
+        for d in range(1, 4):
+            c = copy(g.at[pl.ds(t, 4)], g.at[pl.ds(t, 4)], ss.at[3, color, d - 1], rs.at[3, color, d - 1], along[color][d - 1])
+            c.start()
+            stage.append(c)
+    for c in stage:
+        c.wait_recv()
+    pending += stage
+    c = copy(g.at[pl.ds(base, 32)], g.at[pl.ds(base, 32)], ps.at[2], pr.at[2], partner)
+    c.start()
+    c.wait_recv()
+    pending.append(c)
+    for lb in range(2):
+        for rb in range(32):
+            for p in range(2):
+                out_ref[p, rb * 8 : rb * 8 + 8, lb * 128 : lb * 128 + 128] = g[lb * 32 + rb, p]
+    for c in pending:
+        c.wait_send()
+    for color in range(2):
+
+        @pl.when(z != root(color))
+        def _():
+            pltpu.make_async_copy(s2.at[color], s2.at[color], zs.at[color, 0]).wait()
+            pltpu.make_async_copy(wp.at[3], wp.at[3], zs.at[color, 1]).wait()
+
+        @pl.when(z == root(color))
+        def _():
+            t = slot(color)
+
+            def done(i, carry):
+                pltpu.make_async_copy(g.at[t], g.at[t], gs.at[i]).wait()
+                return carry
+
+            lax.fori_loop(0, 15, done, 0)
+
+
+def reduce_probe(pieces, probe_tiles):
+    tile = (8, 128)
+    dma = pltpu.SemaphoreType.DMA
+    vmem = pltpu.VMEM
+    f32 = jnp.float32
+    return pl.pallas_call(
+        reduce_kernel,
+        out_shape=jax.ShapeDtypeStruct((2, 256, 256), f32),
+        in_specs=[pl.BlockSpec(memory_space=pltpu.VMEM)] * 2,
+        out_specs=pl.BlockSpec(memory_space=pltpu.VMEM),
+        scratch_shapes=[
+            vmem((32, 3) + tile, f32),
+            vmem((32, 3) + tile, f32),
+            vmem((2, 3, 4, 3) + tile, f32),
+            vmem((2, 4, 3) + tile, f32),
+            vmem((2, 3, 3) + tile, f32),
+            vmem((2, 3) + tile, f32),
+            vmem((15, 3) + tile, f32),
+            vmem((64, 2) + tile, f32),
+            vmem((4,) + tile, f32),
+            vmem((7,) + tile, f32),
+            vmem((15,) + tile, f32),
+            dma((3,)),
+            dma((3,)),
+            dma((4, 2, 3)),
+            dma((4, 2, 3)),
+            dma((2, 3)),
+            dma((2, 3)),
+            dma((2, 2)),
+            dma((2,)),
+            dma((15,)),
+            dma((2,)),
+        ],
+        compiler_params=pltpu.CompilerParams(collective_id=0, has_side_effects=True),
+        name="reduce_probe",
+    )(pieces, probe_tiles)
+
+
+def to_tiles(planes):
+    count = planes.shape[0]
+    return planes.reshape(count, 32, 8, 2, 128).transpose(3, 1, 0, 2, 4).reshape(64, count, 8, 128)
 
 
 def extended_2(block, sides, width):
@@ -115,11 +351,7 @@
         jnp.sum(patch_real * diff_imag - patch_imag * diff_real, 0),
         jnp.sum(live * (patch_real * patch_real + patch_imag * patch_imag), 0),
     )
-    sum_real, sum_imag, weight = lax.psum(
-        (local_terms[0], local_terms[1], local_terms[2]), ("row", "col")
-    )
-    denominator = weight + probe_damping * jnp.mean(weight)
-    probe_next = probe_field + jnp.stack([sum_real, sum_imag]) / denominator
+    probe_next = reduce_probe(to_tiles(jnp.stack(local_terms)), to_tiles(probe_field))
     return (specimen_next, probe_next)
 
 

time: 656 us -> 229 us (0.35)
  waiting for transfers between devices: 517 us -> 23.8 us
  Pallas kernels: 0 us -> 80.1 us
  between operations: 15.8 us -> 1.76 us
    psum x1 -> x0, waiting for transfers between devices: 494 us -> none  [shards(): lax.psum((local_terms[0], local_terms[1], local_terms[2]), ('row', 'col'))]
    pallas_call x0 -> x1, Pallas kernels: none -> 80.1 us  [reduce_probe(): pl.pallas_call(reduce_kernel, out_shape=jax.ShapeDtypeStruct((2, 256, 256...]
  transfers between devices with their start and end apart: 9 -> 8, of which waited for: 4 -> 3; matrix products, arithmetic and copies ran while one was open for 2% -> 3% of each run, Pallas kernels for 0% -> 35%
where the time goes in v1:
time: 229 us; the launch traced here: 228 us
  Pallas kernels  80.1 us (35%)
  local copies, waits for them, and re-layouts  42.7 us (19%)
  matrix products  32.3 us (14%)
  starting transfers between devices  28.7 us (13%)
  waiting for transfers between devices  23.8 us (10%)
  other arithmetic  11.1 us (5%)
  loops' own time  7.85 us (3%)
    pallas_call x1, Pallas kernels, reduce_probe(): pl.pallas_call(reduce_kernel, out_shape=jax.ShapeDtypeStruct((2, 256, 256...  80.1 us
    dynamic_update_slice x2, local copies, waits for them, and re-layouts, place(): return lax.dynamic_update_slice(total, current + pieces[slot], start)  21.4 us
    ppermute x4, waiting for transfers between devices, extended_2(): lax.ppermute(lax.slice_in_dim(block, block.shape[dim] - width, None, axis...  19.6 us
    ppermute x4, starting transfers between devices, extended_2(): lax.ppermute(lax.slice_in_dim(block, block.shape[dim] - width, None, axis...  18.6 us
    dot_general x8, matrix products, matmul_left(): jnp.einsum('kj,sjl->skl', table, right, precision=lax.Precision.HIGHEST)  18.1 us
    dot_general x8, matrix products, matmul_right(): jnp.einsum('sjm,ml->sjl', left, table, precision=lax.Precision.HIGHEST)  14.2 us
    ppermute x4, starting transfers between devices, extended_2(): lax.ppermute(lax.slice_in_dim(block, 0, width, axis=dim), axis, backward)  10.1 us
    another operation x1, loops' own time, shards(): buffer = lax.fori_loop(0, slots, place, start_total)  7.83 us
  transfers between devices with their start and end apart: 8, of which 3 were waited for; matrix products, arithmetic and copies ran while one was open for 3% of the time, Pallas kernels for 35%

profile of v1, /device:TPU:1, one launch (start us, length us, event | category | flops | bytes accessed | tf_op | source)
XLA Modules:
  0.0 228.2 jit_solution(13999072411068002771)
XLA Ops:
  0.7 4.6 %collective-permute-start = (f32[2,128,256]{2,1,0:T(8,128)}, f32[2,128,256]{2,1,0:T(8,128)S(1)}, u32[]{:S(2)}, u32[]{:S(2)}) collective-permute-start(f32[2,128,256]{2,1,0:T(8,128)} %param.19), channel_id=1, source_target_pairs={{0,32},{32,64},{64,96},{96,128},{128,160},{160,192},{192,224},{224... | collective-permute-start | bytes 786440 | tf_op jit(solution)/shard_map/ppermute | solution.py:254
  5.3 5.6 %collective-permute-start.1 = (f32[2,128,256]{2,1,0:T(8,128)}, f32[2,128,256]{2,1,0:T(8,128)S(1)}, u32[]{:S(2)}, u32[]{:S(2)}) collective-permute-start(f32[2,128,256]{2,1,0:T(8,128)} %param.19), channel_id=1, source_target_pairs={{32,0},{64,32},{96,64},{128,96},{160,128},{192,160},{224,192},{256... | collective-permute-start | bytes 786440 | tf_op jit(solution)/shard_map/ppermute | solution.py:257
  10.9 1.1 slice_bitcast_fusion.1
  12.4 1.3 dynamic_slice.35
  13.8 1.0 fusion.147
  14.7 2.7 %collective-permute-start.2 = (f32[2,384,128]{2,1,0:T(8,128)}, f32[2,384,128]{2,1,0:T(8,128)S(1)}, u32[]{:S(2)}, u32[]{:S(2)}) collective-permute-start(f32[2,384,128]{2,1,0:T(8,128)} %get-tuple-element.214), channel_id=1, source_target_pairs={{0,1},{1,2},{2,3},{3,4},{4,5},{5,6},{6,7},{7,8},{8,9},{9,10},{10,1... | collective-permute-start | bytes 1179656 | tf_op jit(solution)/shard_map/ppermute | solution.py:254
  17.4 1.3 collective-permute-start.3
  19.4 1.0 copy.33
  20.6 12.7 %collective-permute-done.2 = f32[2,384,128]{2,1,0:T(8,128)S(1)} collective-permute-done((f32[2,384,128]{2,1,0:T(8,128)}, f32[2,384,128]{2,1,0:T(8,128)S(1)}, u32[]{:S(2)}, u32[]{:S(2)}) %collective-permute-start.2) | collective-permute-done | bytes 393248 | tf_op jit(solution)/shard_map/ppermute | solution.py:254
  34.0 1.3 pad_maximum_fusion
  35.3 5.9 %while.21 = (s32[]{:T(128)}, f32[2,384,512]{2,1,0:T(8,128)S(1)}, s32[2,3]{1,0:T(2,128)S(1)}, f32[2,2,256,256]{3,2,0,1:T(8,128)}, s32[]{:T(128)}) while((s32[]{:T(128)}, f32[2,384,512]{2,1,0:T(8,128)S(1)}, s32[2,3]{1,0:T(2,128)S(1)}, f32[2,2,256,256]{3,2,0,1:T(8,128)}, s32[]{:T(128)}) %tuple.85), condition=%wide.while_cond.4, body=%wide.while_body.4.sunk | while | flops 2 | bytes 1050217 | solution.py:314
  36.0 2.2 bitcast_dynamic-update-slice_fusion.2
  38.9 2.3 bitcast_dynamic-update-slice_fusion.2
  41.2 2.9 %fusion.48 = f32[2,256,256]{2,1,0:T(8,128)S(1)} fusion(f32[2,2,256,256]{3,2,0,1:T(8,128)} %get-tuple-element.168, f32[256,256]{1,0:T(8,128)S(1)} %get-tuple-element.218, f32[256,256]{1,0:T(8,128)S(1)} %get-tuple-element.216), kind=kOutput, calls=%fused_computation.82 | convolution fusion | flops 404029440 | bytes 2097152 | tf_op jit(solution)/shard_map/sjm,ml->sjl/dot_general | solution.py:271
  44.1 1.6 fusion.52
  45.6 1.6 convolution_subtract_fusion.1
  47.2 1.8 fusion.46
  49.1 1.6 convolution_add_fusion.1
  50.7 1.8 fusion.50
  52.5 2.0 fusion.8
  54.5 2.0 fusion.24
  56.5 1.6 fusion.40
  58.1 1.6 fusion.44
  59.8 1.7 fusion.5
  61.4 1.7 fusion.6
  63.1 1.6 fusion.42
  64.7 2.6 %fusion.38 = f32[2,256,256]{1,2,0:T(8,128)} fusion(f32[2,256,256]{1,2,0:T(8,128)S(1)} %fusion.5), kind=kOutput, calls=%fused_computation.72 | convolution fusion | flops 403636224 | bytes 1048576 | tf_op jit(solution)/shard_map/kj,sjl->skl/dot_general | solution.py:275
  67.3 2.4 %fusion.4 = f32[2,256,256]{2,1,0:T(8,128)} fusion(f32[2,256,256]{2,1,0:T(8,128)S(1)} %fusion.42, f32[2,256,256]{1,2,0:T(8,128)S(1)} %fusion.5, f32[2]{0:T(128)S(1)} %compare_convert_fusion), kind=kOutput, calls=%fused_computation.11 | convolution fusion | flops 404029440 | bytes 1572872 | tf_op jit(solution)/shard_map/kj,sjl->skl/dot_general | solution.py:275
  69.7 1.2 copy.45
  70.9 4.0 %fusion.15 = (f32[256,256]{1,0:T(8,128)}, f32[256,256]{1,0:T(8,128)}, f32[256,256]{1,0:T(8,128)}, f32[2,1,256,256]{3,2,0,1:T(8,128)S(1)}, f32[2,1,256,256]{3,2,0,1:T(8,128)S(1)}) fusion(f32[2,256,256]{1,2,0:T(8,128)S(1)} %copy.45, f32[2,2,256,256]{3,2,0,1:T(8,128)S(1)} %copy-done.4, f32[2]{0:T(128)S(1)} %compare_convert_fusion, ...), kind=kOutput, calls=%fused_computation.36 | convolution fusion | flops 406323200 | bytes 4981760 | tf_op jit(solution)/shard_map/kj,sjl->skl/dot_general | solution.py:275
  74.9 1.3 pad_maximum_fusion.1
  76.4 34.4 %while.20 = (s32[]{:T(128)}, f32[3,384,512]{2,1,0:T(8,128)S(1)}, s32[2]{0:T(128)S(1)}, s32[2]{0:T(128)S(1)}, f32[2,3,256,256]{3,2,0,1:T(8,128)}, /*index=5*/s32[]{:T(128)}, s32[]{:T(128)}, s32[]{:T(128)}, s32[]{:T(128)}) while((s32[]{:T(128)}, f32[3,384,512]{2,1,0:T(8,128)S(1)}, s32[2]{0:T(128)S(1)}, s32[2]{0:T(128)S(1)}, ...), condition=%wide.region_1.2_spmd, body=%wide.region_0.1_spmd.sunk | while | flops 196616 | bytes 3932361 | solution.py:342
  81.5 1.4 bitcast_add_fusion.2
  83.0 9.7 %dynamic_update_slice.8 = f32[3,384,512]{2,1,0:T(8,128)S(1)} dynamic-update-slice(f32[3,384,512]{2,1,0:T(8,128)S(1)} %get-tuple-element.308, f32[3,256,256]{2,1,0:T(8,128)S(1)} %bitcast_add_fusion.2, s32[]{:T(128)} %constant.191.clone.1..sunk, s32[]{:T(128)S(6)} %select_n.146, s32[]{:T(128)S(6)} %select_n.147) | dynamic-update-slice | bytes 1572868 | tf_op jit(solution)/shard_map/while/body/eval_jaxpr/dynamic_update_slice | solution.py:339
  97.7 1.4 bitcast_add_fusion.2
  99.2 11.6 %dynamic_update_slice.8 = f32[3,384,512]{2,1,0:T(8,128)S(1)} dynamic-update-slice(f32[3,384,512]{2,1,0:T(8,128)S(1)} %get-tuple-element.308, f32[3,256,256]{2,1,0:T(8,128)S(1)} %bitcast_add_fusion.2, s32[]{:T(128)} %constant.191.clone.1..sunk, s32[]{:T(128)S(6)} %select_n.146, s32[]{:T(128)S(6)} %select_n.147) | dynamic-update-slice | bytes 1572868 | tf_op jit(solution)/shard_map/while/body/eval_jaxpr/dynamic_update_slice | solution.py:339
  111.0 7.0 %collective-permute-start.4 = (f32[3,128,512]{2,1,0:T(8,128)S(1)}, f32[3,128,512]{2,1,0:T(8,128)S(1)}, u32[]{:S(2)}, u32[]{:S(2)}) collective-permute-start(f32[3,128,512]{2,1,0:T(8,128)S(1)} %get-tuple-element.207), channel_id=1, source_target_pairs={{0,32},{32,64},{64,96},{96,128},{128,160},{160,192},{192,224},{224... | collective-permute-start | bytes 2359304 | tf_op jit(solution)/shard_map/ppermute | solution.py:254
  118.0 1.9 collective-permute-start.5
  119.9 7.0 %collective-permute-done.4 = f32[3,128,512]{2,1,0:T(8,128)S(1)} collective-permute-done((f32[3,128,512]{2,1,0:T(8,128)S(1)}, f32[3,128,512]{2,1,0:T(8,128)S(1)}, u32[]{:S(2)}, u32[]{:S(2)}) %collective-permute-start.4) | collective-permute-done | bytes 786464 | tf_op jit(solution)/shard_map/ppermute | solution.py:254
  127.2 4.1 %collective-permute-done.5 = f32[3,128,512]{2,1,0:T(8,128)S(1)} collective-permute-done((f32[3,128,512]{2,1,0:T(8,128)S(1)}, f32[3,128,512]{2,1,0:T(8,128)S(1)}, u32[]{:S(2)}, u32[]{:S(2)}) %collective-permute-start.5) | collective-permute-done | bytes 786464 | tf_op jit(solution)/shard_map/ppermute | solution.py:257
  131.4 1.4 fusion.145
  132.9 1.0 copy-done.1
  133.9 4.3 %collective-permute-start.6 = (f32[3,640,128]{2,1,0:T(8,128)}, f32[3,640,128]{2,1,0:T(8,128)S(1)}, u32[]{:S(2)}, u32[]{:S(2)}) collective-permute-start(f32[3,640,128]{2,1,0:T(8,128)} %get-tuple-element.204), channel_id=1, source_target_pairs={{0,1},{1,2},{2,3},{3,4},{4,5},{5,6},{6,7},{7,8},{8,9},{9,10},{10,1... | collective-permute-start | bytes 2949128 | tf_op jit(solution)/shard_map/ppermute | solution.py:254
  138.2 1.3 collective-permute-start.7
  141.7 0.9 copy.50
  142.7 80.1 %reduce_probe.1 = f32[2,256,256]{2,1,0:T(8,128)} custom-call(f32[64,3,8,128]{3,2,1,0:T(8,128)} %bitcast.179, f32[64,2,8,128]{3,2,1,0:T(8,128)} %bitcast.180), custom_call_target="tpu_custom_call" | custom-call | tf_op jit(solution)/shard_map/reduce_probe/pallas_call | solution.py:211
  222.8 1.9 fusion.9
  224.7 0.8 copy-done.2
  (63 shorter events, 10.8 us)
Async XLA Ops:
  0.6 11.3 %copy-start = (s32[16,32,2,2]{1,3,2,0:T(2,128)S(1)}, s32[16,32,2,2]{1,3,2,0:T(2,128)}, u32[]{:S(2)}) copy-start(s32[16,32,2,2]{1,3,2,0:T(2,128)} %param.21) | copy-start | bytes 24580
  0.6 13.0 %copy-start.6 = (f32[2,128,256]{2,1,0:T(8,128)S(1)}, f32[2,128,256]{2,1,0:T(8,128)}, u32[]{:S(2)}) copy-start(f32[2,128,256]{2,1,0:T(8,128)} %param.19) | copy-start | bytes 786436
  0.7 13.0 %collective-permute-start = (f32[2,128,256]{2,1,0:T(8,128)}, f32[2,128,256]{2,1,0:T(8,128)S(1)}, u32[]{:S(2)}, u32[]{:S(2)}) collective-permute-start(f32[2,128,256]{2,1,0:T(8,128)} %param.19), channel_id=1, source_target_pairs={{0,32},{32,64},{64,96},{96,128},{128,160},{160,192},{192,224},{224... | collective-permute-start | bytes 786440 | tf_op jit(solution)/shard_map/ppermute | solution.py:254
  5.3 8.4 %collective-permute-start.1 = (f32[2,128,256]{2,1,0:T(8,128)}, f32[2,128,256]{2,1,0:T(8,128)S(1)}, u32[]{:S(2)}, u32[]{:S(2)}) collective-permute-start(f32[2,128,256]{2,1,0:T(8,128)} %param.19), channel_id=1, source_target_pairs={{32,0},{64,32},{96,64},{128,96},{160,128},{192,160},{224,192},{256... | collective-permute-start | bytes 786440 | tf_op jit(solution)/shard_map/ppermute | solution.py:257
  13.7 5.7 %copy-start.11 = (f32[1,1,2,256,256]{4,3,2,1,0:T(8,128)S(1)}, f32[1,1,2,256,256]{4,3,2,1,0:T(8,128)}, u32[]{:S(2)}) copy-start(f32[1,1,2,256,256]{4,3,2,1,0:T(8,128)} %param.23) | copy-start | bytes 1572868
  14.7 18.5 %collective-permute-start.2 = (f32[2,384,128]{2,1,0:T(8,128)}, f32[2,384,128]{2,1,0:T(8,128)S(1)}, u32[]{:S(2)}, u32[]{:S(2)}) collective-permute-start(f32[2,384,128]{2,1,0:T(8,128)} %get-tuple-element.214), channel_id=1, source_target_pairs={{0,1},{1,2},{2,3},{3,4},{4,5},{5,6},{6,7},{7,8},{8,9},{9,10},{10,1... | collective-permute-start | bytes 1179656 | tf_op jit(solution)/shard_map/ppermute | solution.py:254
  17.4 16.6 %collective-permute-start.3 = (f32[2,384,128]{2,1,0:T(8,128)}, f32[2,384,128]{2,1,0:T(8,128)}, u32[]{:S(2)}, u32[]{:S(2)}) collective-permute-start(f32[2,384,128]{2,1,0:T(8,128)} %get-tuple-element.215), channel_id=1, source_target_pairs={{1,0},{2,1},{3,2},{4,3},{5,4},{6,5},{7,6},{8,7},{9,8},{10,9},{11,1... | collective-permute-start | bytes 1179656 | tf_op jit(solution)/shard_map/ppermute | solution.py:257
  33.2 0.8 copy-start.13
  41.2 2.9 %copy-start.4 = (f32[2,2,256,256]{3,2,0,1:T(8,128)S(1)}, f32[2,2,256,256]{3,2,0,1:T(8,128)}, u32[]{:S(2)}) copy-start(f32[2,2,256,256]{3,2,0,1:T(8,128)} %get-tuple-element.168) | copy-start | bytes 3145732
  50.7 3.8 %copy-start.12 = (f32[1,1,2,256,256]{3,4,2,1,0:T(8,128)S(1)}, f32[1,1,2,256,256]{3,4,2,1,0:T(8,128)}, u32[]{:S(2)}) copy-start(f32[1,1,2,256,256]{3,4,2,1,0:T(8,128)} %copy.33) | copy-start | bytes 1572868
  111.0 15.9 %collective-permute-start.4 = (f32[3,128,512]{2,1,0:T(8,128)S(1)}, f32[3,128,512]{2,1,0:T(8,128)S(1)}, u32[]{:S(2)}, u32[]{:S(2)}) collective-permute-start(f32[3,128,512]{2,1,0:T(8,128)S(1)} %get-tuple-element.207), channel_id=1, source_target_pairs={{0,32},{32,64},{64,96},{96,128},{128,160},{160,192},{192,224},{224... | collective-permute-start | bytes 2359304 | tf_op jit(solution)/shard_map/ppermute | solution.py:254
  118.0 13.3 %collective-permute-start.5 = (f32[3,128,512]{2,1,0:T(8,128)S(1)}, f32[3,128,512]{2,1,0:T(8,128)S(1)}, u32[]{:S(2)}, u32[]{:S(2)}) collective-permute-start(f32[3,128,512]{2,1,0:T(8,128)S(1)} %get-tuple-element.206), channel_id=1, source_target_pairs={{32,0},{64,32},{96,64},{128,96},{160,128},{192,160},{224,192},{256... | collective-permute-start | bytes 2359304 | tf_op jit(solution)/shard_map/ppermute | solution.py:257
  131.4 2.5 %copy-start.1 = (f32[3,640,512]{2,1,0:T(8,128)}, f32[3,640,512]{2,1,0:T(8,128)S(1)}, u32[]{:S(2)}) copy-start(f32[3,640,512]{2,1,0:T(8,128)S(1)} %constant_dynamic-update-slice_fusion.3) | copy-start | bytes 11796484
  131.4 8.1 %copy-start.3 = (f32[2,256,256]{2,1,0:T(8,128)S(1)}, f32[2,256,256]{2,1,0:T(8,128)}, u32[]{:S(2)}) copy-start(f32[2,256,256]{2,1,0:T(8,128)} %param.20) | copy-start | bytes 1572868
  133.9 7.8 %copy-start.8 = (f32[256,256]{1,0:T(8,128)S(1)}, f32[256,256]{1,0:T(8,128)}, u32[]{:S(2)}) copy-start(f32[256,256]{1,0:T(8,128)} %get-tuple-element.179) | copy-start | bytes 786436
  133.9 7.8 %copy-start.9 = (f32[256,256]{1,0:T(8,128)S(1)}, f32[256,256]{1,0:T(8,128)}, u32[]{:S(2)}) copy-start(f32[256,256]{1,0:T(8,128)} %get-tuple-element.180) | copy-start | bytes 786436
  133.9 7.8 %copy-start.10 = (f32[256,256]{1,0:T(8,128)S(1)}, f32[256,256]{1,0:T(8,128)}, u32[]{:S(2)}) copy-start(f32[256,256]{1,0:T(8,128)} %get-tuple-element.181) | copy-start | bytes 786436
  133.9 88.9 %collective-permute-start.6 = (f32[3,640,128]{2,1,0:T(8,128)}, f32[3,640,128]{2,1,0:T(8,128)S(1)}, u32[]{:S(2)}, u32[]{:S(2)}) collective-permute-start(f32[3,640,128]{2,1,0:T(8,128)} %get-tuple-element.204), channel_id=1, source_target_pairs={{0,1},{1,2},{2,3},{3,4},{4,5},{5,6},{6,7},{7,8},{8,9},{9,10},{10,1... | collective-permute-start | bytes 2949128 | tf_op jit(solution)/shard_map/ppermute | solution.py:254
  138.2 84.6 %collective-permute-start.7 = (f32[3,640,128]{2,1,0:T(8,128)}, f32[3,640,128]{2,1,0:T(8,128)S(1)}, u32[]{:S(2)}, u32[]{:S(2)}) collective-permute-start(f32[3,640,128]{2,1,0:T(8,128)} %get-tuple-element.205), channel_id=1, source_target_pairs={{1,0},{2,1},{3,2},{4,3},{5,4},{6,5},{7,6},{8,7},{9,8},{10,9},{11,1... | collective-permute-start | bytes 2949128 | tf_op jit(solution)/shard_map/ppermute | solution.py:257
  222.8 2.8 %copy-start.2 = (f32[3,640,512]{2,1,0:T(8,128)S(1)}, f32[3,640,512]{2,1,0:T(8,128)}, u32[]{:S(2)}) copy-start(f32[3,640,512]{2,1,0:T(8,128)} %copy-done.1) | copy-start | bytes 11796484
  225.7 1.0 copy-start.7
  225.7 1.7 copy-start.5

commit v2 on v1

v2 whole, which is shorter than its diff:
```python
import math

import jax
import jax.numpy as jnp
import numpy as np
from jax import lax
from jax.experimental import pallas as pl
from jax.experimental.pallas import tpu as pltpu
from jax.sharding import PartitionSpec as P

MESH = pl.DeviceIdType.MESH
ROWS = 16
COLS = 32
object_damping = 0.1
probe_damping = 0.1
f32 = jnp.float32
bf16 = jnp.bfloat16
VMEM = pl.BlockSpec(memory_space=pltpu.VMEM)
SMEM = pl.BlockSpec(memory_space=pltpu.SMEM)


def remote(src, dst, send, recv, where):
    return pltpu.make_async_remote_copy(src_ref=src, dst_ref=dst, send_sem=send, recv_sem=recv, device_id=where, device_id_type=MESH)


def greet(barrier, where):
    pl.semaphore_signal(barrier, inc=1, device_id=where, device_id_type=MESH)


def halo_kernel(tile_ref, ext, own, cs, cr, vs, vr):
    row = lax.axis_index("row")
    col = lax.axis_index("col")
    has = {"l": col > 0, "r": col < COLS - 1, "u": row > 0, "d": row < ROWS - 1}
    to = {"l": (row, col - 1), "r": (row, col + 1), "u": (row - 1, col), "d": (row + 1, col)}
    center = [pltpu.make_async_copy(tile_ref.at[:, :, pl.ds(j * 128, 128)], ext.at[:, 1 + j, pl.ds(128, 128), :], own.at[j]) for j in range(2)]
    for c in center:
        c.start()
    barrier = pltpu.get_barrier_semaphore()
    for side in "lrud":

        @pl.when(has[side])
        def _():
            greet(barrier, to[side])

    expected = sum(has[side].astype(jnp.int32) for side in "lrud")

    @pl.when(row == 0)
    def _():
        ext[:, :, 0:128, :] = jnp.zeros((2, 4, 128, 128), f32)

    @pl.when(row == ROWS - 1)
    def _():
        ext[:, :, 256:384, :] = jnp.zeros((2, 4, 128, 128), f32)

    @pl.when(col == 0)
    def _():
        ext[:, 0] = jnp.zeros((2, 384, 128), f32)

    @pl.when(col == COLS - 1)
    def _():
        ext[:, 3] = jnp.zeros((2, 384, 128), f32)

    for c in center:
        c.wait()
    pl.semaphore_wait(barrier, expected)

    def across(p, side):
        mine, theirs = (1, 3) if side == "l" else (2, 0)
        i = 0 if side == "l" else 1
        return remote(ext.at[p, mine, pl.ds(128, 128)], ext.at[p, theirs, pl.ds(128, 128)], cs.at[p, i], cr.at[p, i], to[side])

    def up_down(p, side, part):
        at = (pl.ds(1, 2), 0, 3)[part]
        i, theirs = (0, 256) if side == "u" else (1, 0)
        return remote(ext.at[p, at, pl.ds(128, 128)], ext.at[p, at, pl.ds(theirs, 128)], vs.at[p, part, i], vr.at[p, part, i], to[side])

    for p in range(2):
        for side in "lr":

            @pl.when(has[side])
            def _():
                across(p, side).start()

    for p in range(2):
        for side in "ud":

            @pl.when(has[side])
            def _():
                up_down(p, side, 0).start()

    for p in range(2):
        for side, part in (("l", 1), ("r", 2)):

            @pl.when(has[side])
            def _():
                across(p, "r" if side == "l" else "l").wait_recv()
                for way in "ud":

                    @pl.when(has[way])
                    def _():
                        up_down(p, way, part).start()

    for p in range(2):
        for side in "lr":

            @pl.when(has[side])
            def _():
                across(p, side).wait_send()

        for way, back in (("u", "d"), ("d", "u")):
            for part, need in ((0, None), (1, "l"), (2, "r")):
                cond = has[way] if need is None else jnp.logical_and(has[way], has[need])

                @pl.when(cond)
                def _():
                    up_down(p, way, part).wait_send()
                    up_down(p, back, part).wait_recv()


def halo(tile):
    dma = pltpu.SemaphoreType.DMA
    return pl.pallas_call(
        halo_kernel,
        out_shape=jax.ShapeDtypeStruct((2, 4, 384, 128), f32),
        in_specs=[pl.BlockSpec(memory_space=pl.ANY)],
        out_specs=VMEM,
        scratch_shapes=[dma((2,)), dma((2, 2)), dma((2, 2)), dma((2, 3, 2)), dma((2, 3, 2))],
        compiler_params=pltpu.CompilerParams(collective_id=1, has_side_effects=True),
        name="halo",
    )(tile)


def dft_tables():
    m = np.arange(128)[:, None]
    k = np.arange(128)[None, :]
    tables = []
    for odd in range(2):
        angle = ((m * (2 * k + odd)) % 256) * (2.0 * math.pi / 256)
        c, s = np.cos(angle) / 16, np.sin(angle) / 16
        full = np.block([[c, -s], [s, c]])
        for t in (full, full.T):
            high = t.astype(np.float32).astype(jnp.bfloat16)
            low = (t - high.astype(np.float64)).astype(np.float32).astype(jnp.bfloat16)
            tables += [high, low]
    order = np.concatenate([np.arange(0, 256, 2), np.arange(1, 256, 2)])
    select = (np.arange(256)[:, None] == order[None, :]).astype(jnp.bfloat16)
    return np.stack(tables).reshape(2, 2, 2, 256, 256), select


def split(value):
    high = value.astype(bf16)
    return high, (value - high.astype(f32)).astype(bf16)


def product(a, b):
    def dot(u, v):
        return jnp.dot(u, v, preferred_element_type=f32)

    return dot(a[0], b[0]) + (dot(a[1], b[0]) + dot(a[0], b[1]))


STEP = 64


def tile_kernel(offs, live, ext, probe, mags, tables, select, upd, pieces, den, pat, wave, freq, zb, padded, seen, sems):
    row = lax.axis_index("row")
    col = lax.axis_index("col")

    def table(odd, turned):
        return tables[odd, turned, 0], tables[odd, turned, 1]

    fetch = [[pltpu.make_async_copy(mags.at[0, 0, s, :, pl.ds(j * 128, 128)], seen.at[s, j], sems.at[s, j]) for j in range(2)] for s in range(2)]
    for pair in fetch:
        for c in pair:
            c.start()
    upd[...] = jnp.zeros_like(upd)
    for s in range(2):
        top = offs[(row * 2 + s) * 2, col] + 128
        left = offs[(row * 2 + s) * 2 + 1, col] + 128
        turn, block = left % 128, left // 128
        lane = lax.broadcasted_iota(jnp.int32, (STEP, 128), 1)
        alive = (s < live[row, col]).astype(f32)
        for i in range(0, 256, STEP):
            got = []
            for p in range(2):
                rolled = [pltpu.roll(ext[p, jnp.minimum(block + j, 3), pl.ds(top + i, STEP), :], 128 - turn, 1) for j in range(3)]
                halves = [jnp.where(lane < 128 - turn, rolled[j], rolled[j + 1]) for j in range(2)]
                got.append(jnp.concatenate(halves, 1))
                pat[p, i : i + STEP, :] = got[p]
            pr, pi = probe[0, i : i + STEP, :], probe[1, i : i + STEP, :]
            wr = pr * got[0] - pi * got[1]
            wi = pr * got[1] + pi * got[0]
            for odd in range(2):
                if odd:
                    mixed = [w[:, :128] - w[:, 128:] for w in (wr, wi)]
                else:
                    mixed = [w[:, :128] + w[:, 128:] for w in (wr, wi)]
                out = product(split(jnp.concatenate(mixed, 1)), table(odd, 0))
                for p in range(2):
                    wave[p, i : i + STEP, odd * 128 : odd * 128 + 128] = out[:, p * 128 : p * 128 + 128]
        for odd in range(2):
            if odd:
                mixed = [wave[p, 0:128, :] - wave[p, 128:256, :] for p in range(2)]
            else:
                mixed = [wave[p, 0:128, :] + wave[p, 128:256, :] for p in range(2)]
            freq[odd] = product(table(odd, 1), split(jnp.concatenate(mixed, 0)))
        for c in fetch[s]:
            c.wait()
        for odd in range(2):
            for i in range(0, 128, STEP):
                mh, ml = split(jnp.concatenate([seen[s, j, pl.ds(odd + 2 * i, STEP, stride=2), :] for j in range(2)], 1))
                measured = jnp.dot(mh, select[...], preferred_element_type=f32) + jnp.dot(ml, select[...], preferred_element_type=f32)
                fr = freq[odd, i : i + STEP, :]
                fi = freq[odd, 128 + i : 128 + i + STEP, :]
                factor = measured * lax.rsqrt(jnp.maximum(fr * fr + fi * fi, 0.0625)) - 1.0
                factor = factor * alive
                for p, value in ((0, fr * factor), (1, fi * factor)):
                    high, low = split(value)
                    zb[odd, 0, p * 128 + i : p * 128 + i + STEP, :] = high
                    zb[odd, 1, p * 128 + i : p * 128 + i + STEP, :] = low
        for odd in range(2):
            freq[odd] = product(table(odd, 0), (zb[odd, 0], zb[odd, 1]))
        for p in range(2):
            e = freq[0, p * 128 : p * 128 + 128, :]
            o = freq[1, p * 128 : p * 128 + 128, :]
            wave[p, 0:128, :] = e + o
            wave[p, 128:256, :] = e - o
        for i in range(0, 256, STEP):
            parts = []
            for odd in range(2):
                mixed = [wave[p, i : i + STEP, odd * 128 : odd * 128 + 128] for p in range(2)]
                parts.append(product(split(jnp.concatenate(mixed, 1)), table(odd, 1)))
            diff = []
            for p in range(2):
                e, o = (parts[odd][:, p * 128 : p * 128 + 128] for odd in range(2))
                diff.append(jnp.concatenate([e + o, e - o], 1))
            dr, di = diff
            pr, pi = probe[0, i : i + STEP, :], probe[1, i : i + STEP, :]
            ore, oim = pat[0, i : i + STEP, :], pat[1, i : i + STEP, :]
            for p, grad in ((0, pr * dr + pi * di), (1, pr * di - pi * dr)):
                first, second = (pltpu.roll(grad[:, j * 128 : j * 128 + 128], turn, 1) for j in range(2))
                moved = (jnp.where(lane >= turn, first, 0.0), jnp.where(lane >= turn, second, first), jnp.where(lane < turn, second, 0.0))
                for j in range(3):
                    at = (p, jnp.minimum(block + j, 3), pl.ds(top + i, STEP))
                    upd[at] = upd[at] + moved[j]
            terms = (ore * dr + oim * di, ore * di - oim * dr, (ore * ore + oim * oim) * alive)
            for lb in range(2):
                for rb in range(STEP // 8):
                    t = lb * 32 + i // 8 + rb
                    for p in range(3):
                        value = terms[p][rb * 8 : rb * 8 + 8, lb * 128 : lb * 128 + 128]
                        pieces[t, p] = value if s == 0 else pieces[t, p] + value
    padded[...] = jnp.zeros_like(padded)
    peak = jnp.zeros((8, 128), f32)
    for i in range(0, 256, STEP):
        power = probe[0, i : i + STEP, :] * probe[0, i : i + STEP, :] + probe[1, i : i + STEP, :] * probe[1, i : i + STEP, :]
        for j in range(2):
            padded[2 + j, 128 + i : 128 + i + STEP, :] = power[:, j * 128 : j * 128 + 128]
        for a in range(0, STEP, 8):
            for b in range(0, 256, 128):
                peak = jnp.maximum(peak, power[a : a + 8, b : b + 128])
    den[...] = jnp.full((128, 256), object_damping, f32) * jnp.max(peak)

    def add(n, carry):
        da = n // 6 - 1
        db = (n // 2) % 3 - 1
        s = n % 2
        a = row + da
        b = col + db
        inside = (a >= 0) & (a < ROWS) & (b >= 0) & (b < COLS)
        a = jnp.clip(a, 0, ROWS - 1)
        b = jnp.clip(b, 0, COLS - 1)
        down = da * 128 + offs[(a * 2 + s) * 2, b]
        across = db * 256 + offs[(a * 2 + s) * 2 + 1, b]
        on = inside & (s < live[a, b]) & (across > -256) & (across < 256)

        @pl.when(on)
        def _():
            turn = (across + 256) % 128
            block = 4 - (across + 256) // 128
            lane = lax.broadcasted_iota(jnp.int32, (STEP, 128), 1)
            for i in range(0, 128, STEP):
                rolled = [pltpu.roll(padded[block + j - 1, pl.ds(i + 128 - down, STEP), :], turn, 1) for j in range(3)]
                for j in range(2):
                    den[i : i + STEP, j * 128 : j * 128 + 128] += jnp.where(lane >= turn, rolled[j + 1], rolled[j])

        return carry

    lax.fori_loop(0, 18, add, 0)


def tile_step(offs, live, ext, probe, mags):
    tables, select = dft_tables()
    out = jax.ShapeDtypeStruct
    vmem = pltpu.VMEM
    return pl.pallas_call(
        tile_kernel,
        out_shape=(out((2, 4, 384, 128), f32), out((64, 3, 8, 128), f32), out((128, 256), f32)),
        in_specs=[SMEM, SMEM, VMEM, VMEM, pl.BlockSpec(memory_space=pl.ANY), VMEM, VMEM],
        out_specs=(VMEM,) * 3,
        scratch_shapes=[
            vmem((2, 256, 256), f32),
            vmem((2, 256, 256), f32),
            vmem((2, 256, 256), f32),
            vmem((2, 2, 256, 256), bf16),
            vmem((6, 512, 128), f32),
            vmem((2, 2, 256, 128), f32),
            pltpu.SemaphoreType.DMA((2, 2)),
        ],
        name="tile_step",
    )(offs, live, ext, probe, mags, jnp.asarray(tables), jnp.asarray(select))


def finish_kernel(d_ref, probe_ref, u_ref, den_ref, spec_ref, spec_out, out_ref, fv, side, fc, hs, hr, es, er, rp, s0, r1, s1, r2, s2, r3, g, wp, rw, r3w, ps, pr, ss, rs, ws, wr, zs, zr, gs, gr):
    row = lax.axis_index("row")
    col = lax.axis_index("col")
    core = row % 2
    x = (row // 2) % 4
    y = (row // 8) * 2 + col % 2
    z = col // 2

    def device(core_of, x_of, y_of, z_of):
        return ((y_of // 2) * 8 + x_of * 2 + core_of, z_of * 2 + y_of % 2)

    copy = remote
    partner = device(1 - core, x, y, z)
    along = (
        [device(core, (x + d) % 4, y, z) for d in range(1, 4)],
        [device(core, x, (y + d) % 4, z) for d in range(1, 4)],
    )
    place = (x, y)
    has = {"l": col > 0, "r": col < COLS - 1, "u": row > 0, "d": row < ROWS - 1}
    beside = {"l": (row, col - 1), "r": (row, col + 1), "u": (row - 1, col), "d": (row + 1, col)}

    barrier = pltpu.get_barrier_semaphore()
    pl.semaphore_signal(barrier, inc=1, device_id=partner, device_id_type=MESH)
    for group in along:
        for peer in group:
            pl.semaphore_signal(barrier, inc=1, device_id=peer, device_id_type=MESH)

    def hail(i, carry):
        greet(barrier, device(core, x, y, (z + i) % 16))
        return carry

    lax.fori_loop(1, 16, hail, 0)
    for side_of in "lrud":

        @pl.when(has[side_of])
        def _():
            greet(barrier, beside[side_of])

    expected = 22 + sum(has[side_of].astype(jnp.int32) for side_of in "lrud")

    for i, side_of in enumerate("ud"):

        @pl.when(jnp.logical_not(has[side_of]))
        def _():
            fv[i] = jnp.zeros((2, 4, 128, 128), f32)

    for i, side_of in enumerate("lr"):

        @pl.when(jnp.logical_not(has[side_of]))
        def _():
            fc[i] = jnp.zeros((2, 128, 128), f32)

    total = d_ref[0, 2]
    for t in range(1, 64):
        total = total + d_ref[t, 2]
    wp[0] = total
    pl.semaphore_wait(barrier, expected)

    def vertical(p, part, side_of):
        at = (0, 3, pl.ds(1, 2))[part]
        i, first = (0, 0) if side_of == "u" else (1, 256)
        return copy(u_ref.at[p, at, pl.ds(first, 128)], fv.at[1 - i, p, at], hs.at[p, part, i], hr.at[p, part, 1 - i], beside[side_of])

    def arrival(p, part, side_of):
        at = (0, 3, pl.ds(1, 2))[part]
        i = 0 if side_of == "u" else 1
        return copy(u_ref.at[p, at, pl.ds(0, 128)], fv.at[i, p, at], hs.at[p, part, i], hr.at[p, part, i], beside[side_of])

    def lateral(p, side_of):
        i = 0 if side_of == "l" else 1
        return copy(side.at[i, p], fc.at[1 - i, p], es.at[p, i], er.at[p, 1 - i], beside[side_of])

    def lateral_in(p, side_of):
        i = 0 if side_of == "l" else 1
        return copy(side.at[i, p], fc.at[i, p], es.at[p, i], er.at[p, i], beside[side_of])


    pending = []
    c = copy(d_ref.at[pl.ds((1 - core) * 32, 32)], rp, ps.at[0], pr.at[0], partner)
    c.start()
    cw = copy(wp.at[0], rw.at[0], ps.at[1], pr.at[1], partner)
    cw.start()
    pending += [c, cw]
    c.wait_recv()
    cw.wait_recv()
    base = core * 32

    def join(t, carry):
        s0[t] = d_ref[base + t] + rp[t]
        return carry

    lax.fori_loop(0, 32, join, 0, unroll=4)
    wp[1] = wp[0] + rw[0]

    stage = []
    for color in range(2):
        for d in range(1, 4):
            to = (place[color] + d) % 4
            c = copy(s0.at[pl.ds(color * 16 + to * 4, 4)], r1.at[color, d - 1], ss.at[0, color, d - 1], rs.at[0, color, d - 1], along[color][d - 1])
            c.start()
            stage.append(c)
    for d in range(1, 4):
        c = copy(wp.at[1], rw.at[d], ws.at[0, d - 1], wr.at[0, d - 1], along[0][d - 1])
        c.start()
        stage.append(c)
    for c in stage:
        c.wait_recv()
    pending += stage
    for color in range(2):
        for b in range(4):
            s1[color, b] = s0[color * 16 + place[color] * 4 + b] + (r1[color, 0, b] + (r1[color, 1, b] + r1[color, 2, b]))
    wp[2] = wp[1] + (rw[1] + (rw[2] + rw[3]))

    stage = []
    for color in range(2):
        other = 1 - color
        for d in range(1, 4):
            to = (place[other] + d) % 4
            c = copy(s1.at[color, to], r2.at[color, d - 1], ss.at[1, color, d - 1], rs.at[1, color, d - 1], along[other][d - 1])
            c.start()
            stage.append(c)
    for d in range(1, 4):
        c = copy(wp.at[2], rw.at[3 + d], ws.at[1, d - 1], wr.at[1, d - 1], along[1][d - 1])
        c.start()
        stage.append(c)
    for part in range(3):
        for p in range(2):
            for side_of in "ud":

                @pl.when(has[side_of])
                def _():
                    vertical(p, part, side_of).start()

    for c in stage:
        c.wait_recv()
    pending += stage
    for color in range(2):
        s2[color] = s1[color, place[1 - color]] + (r2[color, 0] + (r2[color, 1] + r2[color, 2]))
    wp[3] = wp[2] + (rw[4] + (rw[5] + rw[6]))

    def root(color):
        return 2 + 8 * color + 4 * core

    def slot(color):
        return core * 32 + color * 16 + place[color] * 4 + place[1 - color]

    for color in range(2):
        goal = root(color)

        @pl.when(z != goal)
        def _():
            at = (z - goal + 16) % 16
            copy(s2.at[color], r3.at[at - 1], zs.at[color, 0], zr.at[0], device(core, x, y, goal)).start()
            copy(wp.at[3], r3w.at[at - 1], zs.at[color, 1], zr.at[1], device(core, x, y, goal)).start()

    for color in range(2):

        @pl.when(z == root(color))
        def _():
            pltpu.make_async_copy(r3, r3, zr.at[0]).wait()
            pltpu.make_async_copy(r3w, r3w, zr.at[1]).wait()
            full = s2[color]
            weight = wp[3]
            for i in range(15):
                full = full + r3[i]
                weight = weight + r3w[i]
            mean = jnp.sum(weight) * (1.0 / 65536.0)
            scale = full[2] + probe_damping * mean
            t = slot(color)
            rows = pl.ds(pl.multiple_of((t % 32) * 8, 8), 8)
            lanes = pl.ds(pl.multiple_of((t // 32) * 128, 128), 128)
            for p in range(2):
                g[t, p] = probe_ref[p, rows, lanes] + full[p] / scale

            def send(i, carry):
                copy(g.at[t], g.at[t], gs.at[i - 1], gr.at[color], device(core, x, y, (z + i) % 16)).start()
                return carry

            lax.fori_loop(1, 16, send, 0)

    for i, (side_of, at) in enumerate((("l", 0), ("r", 3))):
        for p in range(2):
            for way in "ud":

                @pl.when(has[way])
                def _():
                    arrival(p, i, way).wait_recv()

            @pl.when(has[side_of])
            def _():
                side[i, p] = u_ref[p, at, 128:256, :] + (fv[0, p, at] + fv[1, p, at])
                lateral(p, side_of).start()

    for color in range(2):

        @pl.when(z != root(color))
        def _():
            t = slot(color)
            pltpu.make_async_copy(g.at[t], g.at[t], gr.at[color]).wait()

    stage = []
    for color in range(2):
        other = 1 - color
        t = slot(color)
        for d in range(1, 4):
            c = copy(g.at[t], g.at[t], ss.at[2, color, d - 1], rs.at[2, color, d - 1], along[other][d - 1])
            c.start()
            stage.append(c)
    for c in stage:
        c.wait_recv()
    pending += stage
    stage = []
    for color in range(2):
        t = core * 32 + color * 16 + place[color] * 4
        for d in range(1, 4):
            c = copy(g.at[pl.ds(t, 4)], g.at[pl.ds(t, 4)], ss.at[3, color, d - 1], rs.at[3, color, d - 1], along[color][d - 1])
            c.start()
            stage.append(c)
    for c in stage:
        c.wait_recv()
    pending += stage
    c = copy(g.at[pl.ds(base, 32)], g.at[pl.ds(base, 32)], ps.at[2], pr.at[2], partner)
    c.start()
    c.wait_recv()
    pending.append(c)
    for p in range(2):
        for way in "ud":

            @pl.when(has[way])
            def _():
                arrival(p, 2, way).wait_recv()

        for side_of in "lr":

            @pl.when(has[side_of])
            def _():
                lateral_in(p, side_of).wait_recv()

        for i in range(2):
            at = 1 + i
            update = u_ref[p, at, 128:256, :] + (fv[0, p, at] + fv[1, p, at]) + fc[i, p]
            lanes = slice(i * 128, i * 128 + 128)
            spec_out[p, :, lanes] = spec_ref[p, :, lanes] + update / den_ref[:, lanes]
    for lb in range(2):
        for rb in range(32):
            for p in range(2):
                out_ref[p, rb * 8 : rb * 8 + 8, lb * 128 : lb * 128 + 128] = g[lb * 32 + rb, p]
    for c in pending:
        c.wait_send()
    for p in range(2):
        for way in "ud":

            @pl.when(has[way])
            def _():
                for part in range(3):
                    vertical(p, part, way).wait_send()

        for side_of in "lr":

            @pl.when(has[side_of])
            def _():
                lateral(p, side_of).wait_send()

    for color in range(2):

        @pl.when(z != root(color))
        def _():
            pltpu.make_async_copy(s2.at[color], s2.at[color], zs.at[color, 0]).wait()
            pltpu.make_async_copy(wp.at[3], wp.at[3], zs.at[color, 1]).wait()

        @pl.when(z == root(color))
        def _():
            t = slot(color)

            def done(i, carry):
                pltpu.make_async_copy(g.at[t], g.at[t], gs.at[i]).wait()
                return carry

            lax.fori_loop(0, 15, done, 0)


def finish(upd, pieces, den, specimen, probe_field):
    tile = (8, 128)
    dma = pltpu.SemaphoreType.DMA
    vmem = pltpu.VMEM
    return pl.pallas_call(
        finish_kernel,
        out_shape=(jax.ShapeDtypeStruct((2, 128, 256), f32), jax.ShapeDtypeStruct((2, 256, 256), f32)),
        in_specs=[VMEM] * 5,
        out_specs=(VMEM,) * 2,
        scratch_shapes=[
            vmem((2, 2, 4, 128, 128), f32),
            vmem((2, 2, 128, 128), f32),
            vmem((2, 2, 128, 128), f32),
            dma((2, 3, 2)),
            dma((2, 3, 2)),
            dma((2, 2)),
            dma((2, 2)),
            vmem((32, 3) + tile, f32),
            vmem((32, 3) + tile, f32),
            vmem((2, 3, 4, 3) + tile, f32),
            vmem((2, 4, 3) + tile, f32),
            vmem((2, 3, 3) + tile, f32),
            vmem((2, 3) + tile, f32),
            vmem((15, 3) + tile, f32),
            vmem((64, 2) + tile, f32),
            vmem((4,) + tile, f32),
            vmem((7,) + tile, f32),
            vmem((15,) + tile, f32),
            dma((3,)),
            dma((3,)),
            dma((4, 2, 3)),
            dma((4, 2, 3)),
            dma((2, 3)),
            dma((2, 3)),
            dma((2, 2)),
            dma((2,)),
            dma((15,)),
            dma((2,)),
        ],
        compiler_params=pltpu.CompilerParams(collective_id=0, has_side_effects=True),
        name="finish",
    )(pieces, probe_field, upd, den, specimen)


def shards(specimen, probe_field, scan_offsets, live_counts, magnitudes):
    offs = scan_offsets.transpose(0, 2, 3, 1).reshape(ROWS * 4, COLS)
    ext = halo(specimen)
    upd, pieces, den = tile_step(offs, live_counts, ext, probe_field, magnitudes)
    return finish(upd, pieces, den, specimen, probe_field)


def solution(mesh):
    return jax.shard_map(
        shards,
        mesh=mesh,
        in_specs=(P(None, "row", "col"), P(), P(), P(), P("row", "col", None, None, None)),
        out_specs=(P(None, "row", "col"), P()),
        check_vma=False,
    )
```

time: 229 us -> 90.7 us (0.40)
  local copies, waits for them, and re-layouts: 42.7 us -> 3.54 us
  matrix products: 32.3 us -> 0 us
  starting transfers between devices: 28.7 us -> 0 us
  waiting for transfers between devices: 23.8 us -> 0 us
  other arithmetic: 11.1 us -> 0 us
  loops' own time: 7.85 us -> 0 us
  Pallas kernels: 80.1 us -> 86.2 us
    dot_general x16 -> x0, matrix products: 32.3 us -> none  [the longest x8 18.1 us: matmul_left(): jnp.einsum('kj,sjl->skl', table, right, precision=lax.Precision.HIGHEST)]
    ppermute x8 -> x0, starting transfers between devices: 28.7 us -> none  [the longest x4 18.6 us: extended_2(): lax.ppermute(lax.slice_in_dim(block, block.shape[dim] - width, None, axis...]
    ppermute x8 -> x0, waiting for transfers between devices: 23.8 us -> none  [the longest x4 19.6 us: extended_2(): lax.ppermute(lax.slice_in_dim(block, block.shape[dim] - width, None, axis...]
    dynamic_update_slice x2 -> x0, local copies, waits for them, and re-layouts: 21.4 us -> none  [place(): return lax.dynamic_update_slice(total, current + pieces[slot], start)]
    another operation x2 -> x0, loops' own time: 7.85 us -> none  [the longest x1 7.83 us: shards(): buffer = lax.fori_loop(0, slots, place, start_total)]
    pallas_call x1 -> x3, Pallas kernels: 80.1 us -> 86.2 us  [the longest x1 59.6 us: finish(): pl.pallas_call(finish_kernel, out_shape=(jax.ShapeDtypeStruct((2, 128, 25...]
    gather x6 -> x0, local copies, waits for them, and re-layouts: 5.85 us -> none
    add x4 -> x0, other arithmetic: 5.53 us -> none  [the longest x2 2.85 us: place(): return lax.dynamic_update_slice(total, current + pieces[slot], start)]
  transfers between devices with their start and end apart: 8 -> 0, of which waited for: 3 -> 0; matrix products, arithmetic and copies ran while one was open for 3% -> 0% of each run, Pallas kernels for 35% -> 0%
where the time goes in v2:
time: 90.7 us; the launch traced here: 90.4 us
  Pallas kernels  86.2 us (95%)
  local copies, waits for them, and re-layouts  3.54 us (4%)
    pallas_call x1, Pallas kernels, finish(): pl.pallas_call(finish_kernel, out_shape=(jax.ShapeDtypeStruct((2, 128, 25...  59.6 us
    pallas_call x1, Pallas kernels, halo(): pl.pallas_call(halo_kernel, out_shape=jax.ShapeDtypeStruct((2, 4, 384, 12...  16.4 us
    pallas_call x1, Pallas kernels, tile_step(): pl.pallas_call(tile_kernel, out_shape=(out((2, 4, 384, 128), f32), out((6...  10.2 us
    unnamed x2, local copies, waits for them, and re-layouts  3.54 us

profile of v2, /device:TPU:1, one launch (start us, length us, event | category | flops | bytes accessed | tf_op | source)
XLA Modules:
  0.0 90.4 jit_solution(13609277971596430453)
XLA Ops:
  0.6 16.4 %halo.1.ext = f32[2,4,384,128]{3,2,1,0:T(8,128)} custom-call(f32[2,128,256]{2,1,0:T(8,128)} %spec_ref.1), custom_call_target="tpu_custom_call" | custom-call | tf_op jit(solution)/shard_map/halo/pallas_call | solution.py:122
  17.0 10.2 %tile_step.1 = (f32[2,4,384,128]{3,2,1,0:T(8,128)}, f32[64,3,8,128]{3,2,1,0:T(8,128)}, f32[128,256]{1,0:T(8,128)}) custom-call(s32[64,32]{1,0:T(8,128)} %bitcast.3, s32[16,32]{1,0:T(8,128)} %live.1, f32[2,4,384,128]{3,2,1,0:T(8,128)} %halo.1.ext, f32[2,256,256]{2,1,0:T(8,128)} %probe_ref.1, f32[1,1,2,256,256]{4,3,2,1,0:T(8,128)} %mags.1, ...), custom_call_target="tpu_custom_call" | custom-call | tf_op jit(solution)/shard_map/tile_step/pallas_call | solution.py:296
  27.2 59.6 %finish.1 = (f32[2,128,256]{2,1,0:T(8,128)}, f32[2,256,256]{2,1,0:T(8,128)}) custom-call(f32[64,3,8,128]{3,2,1,0:T(8,128)} %get-tuple-element.5.d_ref, f32[2,256,256]{2,1,0:T(8,128)} %probe_ref.1, f32[2,4,384,128]{3,2,1,0:T(8,128)} %get-tuple-element.6.u_ref, f32[128,256]{1,0:T(8,128)} %get-tuple-element.7.den_ref, f32[2,128,256]{2,1,0:T(8,128)} %spec_ref.1), custom_call_target="tpu_custom_call" | custom-call | tf_op jit(solution)/shard_map/finish/pallas_call | solution.py:599
  86.9 1.7 %copy.11 = f32[2,128,256]{2,1,0:T(8,128)} copy(f32[2,128,256]{2,1,0:T(8,128)} %get-tuple-element.10) | data formatting | bytes 524288
  88.5 1.9 %copy.12 = f32[2,256,256]{2,1,0:T(8,128)} copy(f32[2,256,256]{2,1,0:T(8,128)} %get-tuple-element.11) | data formatting | bytes 1048576

commit v3 on v2

v3 whole, which is shorter than its diff:
```python
import math

import jax
import jax.numpy as jnp
import numpy as np
from jax import lax
from jax.experimental import pallas as pl
from jax.experimental.pallas import tpu as pltpu
from jax.sharding import PartitionSpec as P

MESH = pl.DeviceIdType.MESH
ROWS = 16
COLS = 32
object_damping = 0.1
probe_damping = 0.1
f32 = jnp.float32
bf16 = jnp.bfloat16
VMEM = pl.BlockSpec(memory_space=pltpu.VMEM)
HBM = pl.BlockSpec(memory_space=pltpu.MemorySpace.HBM)
SMEM = pl.BlockSpec(memory_space=pltpu.SMEM)


def remote(src, dst, send, recv, where):
    return pltpu.make_async_remote_copy(src_ref=src, dst_ref=dst, send_sem=send, recv_sem=recv, device_id=where, device_id_type=MESH)


def greet(barrier, where):
    pl.semaphore_signal(barrier, inc=1, device_id=where, device_id_type=MESH)

STEP = 64


def halo_kernel(offs_hbm, live_hbm, tile_ref, probe_hbm, mags, ext, den, probe, seen, padded, offs, live, own, fetch, cs, cr, vs, vr):
    row = lax.axis_index("row")
    col = lax.axis_index("col")
    has = {"l": col > 0, "r": col < COLS - 1, "u": row > 0, "d": row < ROWS - 1}
    to = {"l": (row, col - 1), "r": (row, col + 1), "u": (row - 1, col), "d": (row + 1, col)}
    center = [pltpu.make_async_copy(tile_ref.at[:, :, pl.ds(j * 128, 128)], ext.at[:, 1 + j, pl.ds(128, 128), :], own.at[j]) for j in range(2)]
    for c in center:
        c.start()
    small = [pltpu.make_async_copy(a, b, fetch.at[i]) for i, (a, b) in enumerate(((offs_hbm, offs), (live_hbm, live), (probe_hbm, probe)))]
    for c in small:
        c.start()
    shown = [pltpu.make_async_copy(mags.at[0, 0, s, :, pl.ds(j * 128, 128)], seen.at[s, j], fetch.at[3 + 2 * s + j]) for s in range(2) for j in range(2)]
    barrier = pltpu.get_barrier_semaphore()
    for side in "lrud":

        @pl.when(has[side])
        def _():
            greet(barrier, to[side])

    expected = sum(has[side].astype(jnp.int32) for side in "lrud")

    @pl.when(row == 0)
    def _():
        ext[:, :, 0:128, :] = jnp.zeros((2, 4, 128, 128), f32)

    @pl.when(row == ROWS - 1)
    def _():
        ext[:, :, 256:384, :] = jnp.zeros((2, 4, 128, 128), f32)

    @pl.when(col == 0)
    def _():
        ext[:, 0] = jnp.zeros((2, 384, 128), f32)

    @pl.when(col == COLS - 1)
    def _():
        ext[:, 3] = jnp.zeros((2, 384, 128), f32)

    for c in center:
        c.wait()
    pl.semaphore_wait(barrier, expected)

    def across(p, side):
        mine, theirs = (1, 3) if side == "l" else (2, 0)
        i = 0 if side == "l" else 1
        return remote(ext.at[p, mine, pl.ds(128, 128)], ext.at[p, theirs, pl.ds(128, 128)], cs.at[p, i], cr.at[p, i], to[side])

    def up_down(p, side, part):
        at = (pl.ds(1, 2), 0, 3)[part]
        i, theirs = (0, 256) if side == "u" else (1, 0)
        return remote(ext.at[p, at, pl.ds(128, 128)], ext.at[p, at, pl.ds(theirs, 128)], vs.at[p, part, i], vr.at[p, part, i], to[side])

    for p in range(2):
        for side in "lr":

            @pl.when(has[side])
            def _():
                across(p, side).start()

    for p in range(2):
        for side in "ud":

            @pl.when(has[side])
            def _():
                up_down(p, side, 0).start()

    for c in shown:
        c.start()
    for c in small:
        c.wait()
    padded[...] = jnp.zeros_like(padded)
    peak = jnp.zeros((8, 128), f32)
    for i in range(0, 256, STEP):
        power = probe[0, i : i + STEP, :] * probe[0, i : i + STEP, :] + probe[1, i : i + STEP, :] * probe[1, i : i + STEP, :]
        for j in range(2):
            padded[2 + j, 128 + i : 128 + i + STEP, :] = power[:, j * 128 : j * 128 + 128]
        for a in range(0, STEP, 8):
            for b in range(0, 256, 128):
                peak = jnp.maximum(peak, power[a : a + 8, b : b + 128])
    den[...] = jnp.full((128, 256), object_damping, f32) * jnp.max(peak)

    def add(n, carry):
        da = n // 6 - 1
        db = (n // 2) % 3 - 1
        s = n % 2
        a = row + da
        b = col + db
        inside = (a >= 0) & (a < ROWS) & (b >= 0) & (b < COLS)
        a = jnp.clip(a, 0, ROWS - 1)
        b = jnp.clip(b, 0, COLS - 1)
        down = da * 128 + offs[(a * 2 + s) * 2, b]
        across = db * 256 + offs[(a * 2 + s) * 2 + 1, b]
        on = (inside & (s < live[a, b]) & (across > -256) & (across < 256)).astype(f32)
        across = jnp.clip(across, -256, 255)
        turn = (across + 256) % 128
        block = 4 - (across + 256) // 128
        lane = lax.broadcasted_iota(jnp.int32, (STEP, 128), 1)
        for i in range(0, 128, STEP):
            rolled = [pltpu.roll(padded[block + j - 1, pl.ds(i + 128 - down, STEP), :], turn, 1) for j in range(3)]
            for j in range(2):
                den[i : i + STEP, j * 128 : j * 128 + 128] += on * jnp.where(lane >= turn, rolled[j + 1], rolled[j])

        return carry

    lax.fori_loop(0, 18, add, 0)

    for p in range(2):
        for side, part in (("l", 1), ("r", 2)):

            @pl.when(has[side])
            def _():
                across(p, "r" if side == "l" else "l").wait_recv()
                for way in "ud":

                    @pl.when(has[way])
                    def _():
                        up_down(p, way, part).start()

    for p in range(2):
        for side in "lr":

            @pl.when(has[side])
            def _():
                across(p, side).wait_send()

        for way, back in (("u", "d"), ("d", "u")):
            for part, need in ((0, None), (1, "l"), (2, "r")):
                cond = has[way] if need is None else jnp.logical_and(has[way], has[need])

                @pl.when(cond)
                def _():
                    up_down(p, way, part).wait_send()
                    up_down(p, back, part).wait_recv()

    for c in shown:
        c.wait()


def halo(offs, live, tile, probe, mags):
    dma = pltpu.SemaphoreType.DMA
    return pl.pallas_call(
        halo_kernel,
        out_shape=(jax.ShapeDtypeStruct((2, 4, 384, 128), f32), jax.ShapeDtypeStruct((128, 256), f32), jax.ShapeDtypeStruct((2, 256, 256), f32), jax.ShapeDtypeStruct((2, 2, 256, 128), f32)),
        in_specs=[HBM] * 5,
        out_specs=(VMEM,) * 4,
        scratch_shapes=[pltpu.VMEM((6, 512, 128), f32), pltpu.SMEM((ROWS * 4, COLS), jnp.int32), pltpu.SMEM((ROWS, COLS), jnp.int32), dma((2,)), dma((7,)), dma((2, 2)), dma((2, 2)), dma((2, 3, 2)), dma((2, 3, 2))],
        compiler_params=pltpu.CompilerParams(collective_id=1, has_side_effects=True, vmem_limit_bytes=8 << 20),
        cost_estimate=pl.CostEstimate(flops=400000000, bytes_accessed=1 << 20, transcendentals=0),
        name="halo",
    )(*(pltpu.with_memory_space_constraint(a, pltpu.MemorySpace.HBM) for a in (offs, live, tile, probe, mags)))


def dft_tables():
    m = np.arange(128)[:, None]
    k = np.arange(128)[None, :]
    tables = []
    for odd in range(2):
        angle = ((m * (2 * k + odd)) % 256) * (2.0 * math.pi / 256)
        c, s = np.cos(angle) / 16, np.sin(angle) / 16
        full = np.block([[c, -s], [s, c]])
        for t in (full, full.T):
            high = t.astype(np.float32).astype(jnp.bfloat16)
            low = (t - high.astype(np.float64)).astype(np.float32).astype(jnp.bfloat16)
            tables += [high, low]
    order = np.concatenate([np.arange(0, 256, 2), np.arange(1, 256, 2)])
    select = (np.arange(256)[:, None] == order[None, :]).astype(jnp.bfloat16)
    return np.stack(tables).reshape(2, 2, 2, 256, 256), select


def split(value):
    high = value.astype(bf16)
    return high, (value - high.astype(f32)).astype(bf16)


def product(a, b):
    def dot(u, v):
        return jnp.dot(u, v, preferred_element_type=f32)

    return dot(a[0], b[0]) + (dot(a[1], b[0]) + dot(a[0], b[1]))


def tile_kernel(offs_hbm, live_hbm, ext, probe, seen, tables, select, upd, pieces, pat, wave, freq, zb, measured, offs, live, sems):
    row = lax.axis_index("row")
    col = lax.axis_index("col")

    def table(odd, turned):
        return tables[odd, turned, 0], tables[odd, turned, 1]

    fetch = [pltpu.make_async_copy(a, b, sems.at[i]) for i, (a, b) in enumerate(((offs_hbm, offs), (live_hbm, live)))]
    for c in fetch:
        c.start()
    for s in range(2):
        for odd in range(2):
            for i in range(0, 128, STEP):
                mh, ml = split(jnp.concatenate([seen[s, j, pl.ds(odd + 2 * i, STEP, stride=2), :] for j in range(2)], 1))
                measured[s, odd, i : i + STEP, :] = jnp.dot(mh, select[...], preferred_element_type=f32) + jnp.dot(ml, select[...], preferred_element_type=f32)
    upd[...] = jnp.zeros_like(upd)
    for c in fetch:
        c.wait()
    for s in range(2):
        top = offs[(row * 2 + s) * 2, col] + 128
        left = offs[(row * 2 + s) * 2 + 1, col] + 128
        turn, block = left % 128, left // 128
        lane = lax.broadcasted_iota(jnp.int32, (STEP, 128), 1)
        alive = (s < live[row, col]).astype(f32)
        for i in range(0, 256, STEP):
            got = []
            for p in range(2):
                rolled = [pltpu.roll(ext[p, jnp.minimum(block + j, 3), pl.ds(top + i, STEP), :], 128 - turn, 1) for j in range(3)]
                halves = [jnp.where(lane < 128 - turn, rolled[j], rolled[j + 1]) for j in range(2)]
                got.append(jnp.concatenate(halves, 1))
                pat[p, i : i + STEP, :] = got[p]
            pr, pi = probe[0, i : i + STEP, :], probe[1, i : i + STEP, :]
            wr = pr * got[0] - pi * got[1]
            wi = pr * got[1] + pi * got[0]
            for odd in range(2):
                if odd:
                    mixed = [w[:, :128] - w[:, 128:] for w in (wr, wi)]
                else:
                    mixed = [w[:, :128] + w[:, 128:] for w in (wr, wi)]
                out = product(split(jnp.concatenate(mixed, 1)), table(odd, 0))
                for p in range(2):
                    wave[p, i : i + STEP, odd * 128 : odd * 128 + 128] = out[:, p * 128 : p * 128 + 128]
        for odd in range(2):
            if odd:
                mixed = [wave[p, 0:128, :] - wave[p, 128:256, :] for p in range(2)]
            else:
                mixed = [wave[p, 0:128, :] + wave[p, 128:256, :] for p in range(2)]
            freq[odd] = product(table(odd, 1), split(jnp.concatenate(mixed, 0)))
        for odd in range(2):
            for i in range(0, 128, STEP):
                fr = freq[odd, i : i + STEP, :]
                fi = freq[odd, 128 + i : 128 + i + STEP, :]
                factor = measured[s, odd, i : i + STEP, :] * lax.rsqrt(jnp.maximum(fr * fr + fi * fi, 0.0625)) - 1.0
                factor = factor * alive
                for p, value in ((0, fr * factor), (1, fi * factor)):
                    high, low = split(value)
                    zb[odd, 0, p * 128 + i : p * 128 + i + STEP, :] = high
                    zb[odd, 1, p * 128 + i : p * 128 + i + STEP, :] = low
        for odd in range(2):
            freq[odd] = product(table(odd, 0), (zb[odd, 0], zb[odd, 1]))
        for p in range(2):
            e = freq[0, p * 128 : p * 128 + 128, :]
            o = freq[1, p * 128 : p * 128 + 128, :]
            wave[p, 0:128, :] = e + o
            wave[p, 128:256, :] = e - o
        for i in range(0, 256, STEP):
            parts = []
            for odd in range(2):
                mixed = [wave[p, i : i + STEP, odd * 128 : odd * 128 + 128] for p in range(2)]
                parts.append(product(split(jnp.concatenate(mixed, 1)), table(odd, 1)))
            diff = []
            for p in range(2):
                e, o = (parts[odd][:, p * 128 : p * 128 + 128] for odd in range(2))
                diff.append(jnp.concatenate([e + o, e - o], 1))
            dr, di = diff
            pr, pi = probe[0, i : i + STEP, :], probe[1, i : i + STEP, :]
            ore, oim = pat[0, i : i + STEP, :], pat[1, i : i + STEP, :]
            for p, grad in ((0, pr * dr + pi * di), (1, pr * di - pi * dr)):
                first, second = (pltpu.roll(grad[:, j * 128 : j * 128 + 128], turn, 1) for j in range(2))
                moved = (jnp.where(lane >= turn, first, 0.0), jnp.where(lane >= turn, second, first), jnp.where(lane < turn, second, 0.0))
                for j in range(3):
                    at = (p, jnp.minimum(block + j, 3), pl.ds(top + i, STEP))
                    upd[at] = upd[at] + moved[j]
            terms = (ore * dr + oim * di, ore * di - oim * dr, (ore * ore + oim * oim) * alive)
            for lb in range(2):
                for rb in range(STEP // 8):
                    t = lb * 32 + i // 8 + rb
                    for p in range(3):
                        value = terms[p][rb * 8 : rb * 8 + 8, lb * 128 : lb * 128 + 128]
                        pieces[t, p] = value if s == 0 else pieces[t, p] + value


def tile_step(offs, live, ext, probe, seen):
    tables, select = dft_tables()
    out = jax.ShapeDtypeStruct
    vmem = pltpu.VMEM
    return pl.pallas_call(
        tile_kernel,
        out_shape=(out((2, 4, 384, 128), f32), out((64, 3, 8, 128), f32)),
        in_specs=[HBM, HBM] + [VMEM] * 5,
        out_specs=(VMEM,) * 2,
        scratch_shapes=[
            vmem((2, 256, 256), f32),
            vmem((2, 256, 256), f32),
            vmem((2, 256, 256), f32),
            vmem((2, 2, 256, 256), bf16),
            vmem((2, 2, 128, 256), f32),
            pltpu.SMEM((ROWS * 4, COLS), jnp.int32),
            pltpu.SMEM((ROWS, COLS), jnp.int32),
            pltpu.SemaphoreType.DMA((2,)),
        ],
        compiler_params=pltpu.CompilerParams(vmem_limit_bytes=16 << 20),
        cost_estimate=pl.CostEstimate(flops=400000000, bytes_accessed=1 << 20, transcendentals=0),
        name="tile_step",
    )(*(pltpu.with_memory_space_constraint(a, pltpu.MemorySpace.HBM) for a in (offs, live)), ext, probe, seen, jnp.asarray(tables), jnp.asarray(select))


def finish_kernel(d_ref, probe_ref, u_ref, den_ref, spec_ref, spec_out, g, fv, side, fc, rp, s0, r1, s1, r2, s2, r3, wp, rw, r3w, hs, hr, es, er, ps, pr, ss1, rs1, ss2, rs2, ss3, rs3, ss4, rs4, ws, wr, zs, zr, gs, gr, know):
    row = lax.axis_index("row")
    col = lax.axis_index("col")
    core = row % 2
    x = (row // 2) % 4
    y = (row // 8) * 2 + col % 2
    z = col // 2

    def device(core_of, x_of, y_of, z_of):
        return ((y_of // 2) * 8 + x_of * 2 + core_of, z_of * 2 + y_of % 2)

    def peer(axis, d):
        return device(core, jnp.where(axis == 0, (x + d) % 4, x), jnp.where(axis == 0, y, (y + d) % 4), z)

    partner = device(1 - core, x, y, z)
    place = (x, y)
    has = {"l": col > 0, "r": col < COLS - 1, "u": row > 0, "d": row < ROWS - 1}
    beside = {"l": (row, col - 1), "r": (row, col + 1), "u": (row - 1, col), "d": (row + 1, col)}

    barrier = pltpu.get_barrier_semaphore()
    greet(barrier, partner)
    for axis in range(2):
        for d in range(1, 4):
            greet(barrier, peer(axis, d))

    def along(d):
        return device(core, x, y, (z + d) % 16)

    greet(barrier, along(1))
    greet(barrier, along(15))

    def tell(n, d):
        for way in (d, 16 - d):
            pl.semaphore_signal(know.at[n], inc=1, device_id=along(way), device_id_type=MESH)

    for way in "lrud":

        @pl.when(has[way])
        def _():
            greet(barrier, beside[way])

    expected = 9 + sum(has[way].astype(jnp.int32) for way in "lrud")

    for i, way in enumerate("ud"):

        @pl.when(jnp.logical_not(has[way]))
        def _():
            fv[i] = jnp.zeros((2, 4, 128, 128), f32)

    for i, way in enumerate("lr"):

        @pl.when(jnp.logical_not(has[way]))
        def _():
            fc[i] = jnp.zeros((2, 128, 128), f32)

    total = d_ref[0, 2]
    for t in range(1, 64):
        total = total + d_ref[t, 2]
    wp[0] = total
    pl.semaphore_wait(barrier, expected)
    tell(0, 1)

    def vertical(p, part, way, inward=False):
        at = (0, 3, pl.ds(1, 2))[part]
        i = 0 if way == "u" else 1
        there = i if inward else 1 - i
        return remote(u_ref.at[p, at, pl.ds(256 * i, 128)], fv.at[there, p, at], hs.at[p, part, i], hr.at[p, part, there], beside[way])

    def lateral(p, way, inward=False):
        i = 0 if way == "l" else 1
        there = i if inward else 1 - i
        return remote(side.at[i, p], fc.at[there, p], es.at[p, i], er.at[p, there], beside[way])

    base = core * 32
    pending = []

    def go(c):
        c.start()
        pending.append(c)
        return c

    def spot(color, d):
        return color * 16 + ((place[color] + d) % 4) * 4

    near = (2, 1, 3)
    pairs = {}
    for d in near + (0,):
        for color in range(2):
            at = spot(color, d)
            pairs[color, d] = go(remote(d_ref.at[pl.ds((1 - core) * 32 + at, 4)], rp.at[pl.ds(at, 4)], ps.at[color, d], pr.at[color, d], partner))
        if d == 2:
            first = go(remote(wp.at[0], rw.at[0], ws.at[0], wr.at[0], partner))

    pl.semaphore_wait(know.at[0], 2)
    tell(1, 2)

    def join(color, d):
        pairs[color, d].wait_recv()
        at = spot(color, d)
        for b in range(4):
            s0[at + b] = d_ref[base + at + b] + rp[at + b]

    for d in near:
        for color in range(2):
            join(color, d)
    pl.semaphore_wait(know.at[1], 2)
    tell(2, 4)
    one = {}
    for e in near + (0,):
        for d in near:
            for color in range(2):
                b = (place[1 - color] + e) % 4
                one[color, d, e] = go(remote(s0.at[spot(color, d) + b], r1.at[color, d - 1, e], ss1.at[color, d - 1, e], rs1.at[color, d - 1, e], peer(color, d)))
        if e == 2:
            first.wait_recv()
            wp[1] = wp[0] + rw[0]
            waves = [go(remote(wp.at[1], rw.at[d], ws.at[d], wr.at[d], peer(0, d))) for d in range(1, 4)]
    for color in range(2):
        join(color, 0)
    two = {}
    for e in near + (0,):
        for color in range(2):
            b = (place[1 - color] + e) % 4
            for d in near:
                one[color, d, e].wait_recv()
            s1[color, e] = s0[spot(color, 0) + b] + (r1[color, 0, e] + (r1[color, 1, e] + r1[color, 2, e]))
            if e:
                two[color, e] = go(remote(s1.at[color, e], r2.at[color, e - 1], ss2.at[color, e - 1], rs2.at[color, e - 1], peer(1 - color, e)))
        if e == 2:
            for c in waves:
                c.wait_recv()
            wp[2] = wp[1] + (rw[1] + (rw[2] + rw[3]))
            waves = [go(remote(wp.at[2], rw.at[3 + d], ws.at[3 + d], wr.at[3 + d], peer(1, d))) for d in range(1, 4)]
    for part in range(3):
        for p in range(2):
            for way in "ud":

                @pl.when(has[way])
                def _():
                    vertical(p, part, way).start()

    for c in waves:
        c.wait_recv()
    wp[3] = wp[2] + (rw[4] + (rw[5] + rw[6]))
    pl.semaphore_wait(know.at[2], 2)

    def root(color):
        return 2 + 8 * color + 4 * core

    def slot(color):
        return base + color * 16 + jnp.where(color == 0, x * 4 + y, y * 4 + x)

    for color in range(2):
        for e in near:
            two[color, e].wait_recv()
        s2[color] = s1[color, 0] + (r2[color, 0] + (r2[color, 1] + r2[color, 2]))
        goal = root(color)

        @pl.when(z != goal)
        def _():
            at = (z - goal + 16) % 16
            remote(s2.at[color], r3.at[at - 1], zs.at[color, 0], zr.at[0], device(core, x, y, goal)).start()
            remote(wp.at[3], r3w.at[at - 1], zs.at[color, 1], zr.at[1], device(core, x, y, goal)).start()

    for color in range(2):

        @pl.when(z == root(color))
        def _():
            pltpu.make_async_copy(r3, r3, zr.at[0]).wait()
            pltpu.make_async_copy(r3w, r3w, zr.at[1]).wait()
            full = s2[color]
            weight = wp[3]
            for i in range(15):
                full = full + r3[i]
                weight = weight + r3w[i]
            mean = jnp.sum(weight) * (1.0 / 65536.0)
            scale = full[2] + probe_damping * mean
            t = slot(color)
            rows = pl.ds(pl.multiple_of((t % 32) * 8, 8), 8)
            lanes = pl.ds(pl.multiple_of((t // 32) * 128, 128), 128)
            for p in range(2):
                g[t, p] = probe_ref[p, rows, lanes] + full[p] / scale

            def send(i, carry):
                remote(g.at[t], g.at[t], gs.at[i - 1], gr.at[color], device(core, x, y, (z + i) % 16)).start()
                return carry

            lax.fori_loop(1, 16, send, 0)

    for i, (way, at) in enumerate((("l", 0), ("r", 3))):
        for p in range(2):
            for up_down in "ud":

                @pl.when(has[up_down])
                def _():
                    vertical(p, i, up_down, True).wait_recv()

            @pl.when(has[way])
            def _():
                side[i, p] = u_ref[p, at, 128:256, :] + (fv[0, p, at] + fv[1, p, at])
                lateral(p, way).start()

    def away(color):
        d = (z - root(color) + 16) % 16
        return jnp.minimum(d, 16 - d)

    nearer = (away(1) < away(0)).astype(jnp.int32)
    colors = (nearer, 1 - nearer)

    def own(color):
        return jnp.where(color == 0, x, y)

    def cross(color):
        return jnp.where(color == 0, y, x)

    def tile_at(color, a, b):
        return base + color * 16 + (a % 4) * 4 + b % 4

    three = {}
    four = {}
    for n, color in enumerate(colors):
        t = slot(color)

        @pl.when(z != root(color))
        def _():
            pltpu.make_async_copy(g.at[t], g.at[t], gr.at[color]).wait()

        for d in near:
            three[n, d] = go(remote(g.at[t], g.at[t], ss3.at[color, d - 1], rs3.at[color, d - 1], peer(1 - color, d)))
        for d in near:
            four[n, d, 0] = go(remote(g.at[t], g.at[t], ss4.at[color, d - 1, 0], rs4.at[color, d - 1, 0], peer(color, d)))
    last = []
    for n, color in enumerate(colors):
        for e in (1, 3, 2):
            three[n, e].wait_recv()
            t = tile_at(color, own(color), cross(color) - e + 4)
            for d in near:
                four[n, d, e] = go(remote(g.at[t], g.at[t], ss4.at[color, d - 1, e], rs4.at[color, d - 1, e], peer(color, d)))
        group = g.at[pl.ds(tile_at(color, own(color), 0), 4)]
        last.append(go(remote(group, group, ps.at[2 + n, 0], pr.at[2 + n, 0], partner)))
    for n, color in enumerate(colors):
        for d in (1, 3, 2):
            for e in range(4):
                four[n, d, e].wait_recv()
            group = g.at[pl.ds(tile_at(color, own(color) - d + 4, 0), 4)]
            last.append(go(remote(group, group, ps.at[2 + n, d], pr.at[2 + n, d], partner)))
    for p in range(2):
        for way in "ud":

            @pl.when(has[way])
            def _():
                vertical(p, 2, way, True).wait_recv()

        for way in "lr":

            @pl.when(has[way])
            def _():
                lateral(p, way, True).wait_recv()

        for i in range(2):
            at = 1 + i
            update = u_ref[p, at, 128:256, :] + (fv[0, p, at] + fv[1, p, at]) + fc[i, p]
            lanes = slice(i * 128, i * 128 + 128)
            spec_out[p, :, lanes] = spec_ref[p, :, lanes] + update / den_ref[:, lanes]
    for c in last:
        c.wait_recv()
    for c in pending:
        c.wait_send()
    for p in range(2):
        for way in "ud":

            @pl.when(has[way])
            def _():
                for part in range(3):
                    vertical(p, part, way).wait_send()

        for way in "lr":

            @pl.when(has[way])
            def _():
                lateral(p, way).wait_send()

    for color in range(2):

        @pl.when(z != root(color))
        def _():
            pltpu.make_async_copy(s2.at[color], s2.at[color], zs.at[color, 0]).wait()
            pltpu.make_async_copy(wp.at[3], wp.at[3], zs.at[color, 1]).wait()

        @pl.when(z == root(color))
        def _():
            t = slot(color)

            def done(i, carry):
                pltpu.make_async_copy(g.at[t], g.at[t], gs.at[i]).wait()
                return carry

            lax.fori_loop(0, 15, done, 0)


def finish(upd, pieces, den, specimen, probe_field):
    tile = (8, 128)
    dma = pltpu.SemaphoreType.DMA

    def vmem(*shape):
        return pltpu.VMEM(shape, f32)

    return pl.pallas_call(
        finish_kernel,
        out_shape=(jax.ShapeDtypeStruct((2, 128, 256), f32), jax.ShapeDtypeStruct((64, 2, 8, 128), f32)),
        in_specs=[VMEM] * 5,
        out_specs=(VMEM,) * 2,
        scratch_shapes=[
            vmem(2, 2, 4, 128, 128),
            vmem(2, 2, 128, 128),
            vmem(2, 2, 128, 128),
            vmem(32, 3, *tile),
            vmem(32, 3, *tile),
            vmem(2, 3, 4, 3, *tile),
            vmem(2, 4, 3, *tile),
            vmem(2, 3, 3, *tile),
            vmem(2, 3, *tile),
            vmem(15, 3, *tile),
            vmem(4, *tile),
            vmem(7, *tile),
            vmem(15, *tile),
            dma((2, 3, 2)),
            dma((2, 3, 2)),
            dma((2, 2)),
            dma((2, 2)),
            dma((4, 4)),
            dma((4, 4)),
            dma((2, 3, 4)),
            dma((2, 3, 4)),
            dma((2, 3)),
            dma((2, 3)),
            dma((2, 3)),
            dma((2, 3)),
            dma((2, 3, 4)),
            dma((2, 3, 4)),
            dma((7,)),
            dma((7,)),
            dma((2, 2)),
            dma((2,)),
            dma((15,)),
            dma((2,)),
            pltpu.SemaphoreType.REGULAR((3,)),
        ],
        compiler_params=pltpu.CompilerParams(collective_id=0, has_side_effects=True, vmem_limit_bytes=16 << 20),
        cost_estimate=pl.CostEstimate(flops=1000000000, bytes_accessed=1 << 20, transcendentals=0),
        name="finish",
    )(pieces, probe_field, upd, den, specimen)


def write_kernel(spec_ref, g_ref, spec_out, probe_out):
    spec_out[...] = spec_ref[...]
    for lb in range(2):
        for rb in range(32):
            for p in range(2):
                probe_out[p, rb * 8 : rb * 8 + 8, lb * 128 : lb * 128 + 128] = g_ref[lb * 32 + rb, p]


def write(specimen_next, probe_tiles):
    return pl.pallas_call(
        write_kernel,
        out_shape=(jax.ShapeDtypeStruct((2, 128, 256), f32), jax.ShapeDtypeStruct((2, 256, 256), f32)),
        in_specs=[VMEM] * 2,
        out_specs=(VMEM,) * 2,
        compiler_params=pltpu.CompilerParams(vmem_limit_bytes=8 << 20),
        name="write",
    )(specimen_next, probe_tiles)


def shards(specimen, probe_field, scan_offsets, live_counts, magnitudes):
    offs = scan_offsets.transpose(0, 2, 3, 1).reshape(ROWS * 4, COLS)
    ext, den, probe, seen = halo(offs, live_counts, specimen, probe_field, magnitudes)
    upd, pieces = tile_step(offs, live_counts, ext, probe, seen)
    return write(*finish(upd, pieces, den, specimen, probe))


def solution(mesh):
    return jax.shard_map(
        shards,
        mesh=mesh,
        in_specs=(P(None, "row", "col"), P(), P(), P(), P("row", "col", None, None, None)),
        out_specs=(P(None, "row", "col"), P()),
        check_vma=False,
    )
```

time: 90.7 us -> 74.9 us (0.83)
  Pallas kernels: 86.2 us -> 74 us
  local copies, waits for them, and re-layouts: 3.54 us -> 0.02 us
    pallas_call x1, Pallas kernels: 59.6 us -> 51.8 us  [finish(): pl.pallas_call(finish_kernel, out_shape=(jax.ShapeDtypeStruct((2, 128, 25...]
    pallas_call x1, Pallas kernels: 10.2 us -> 5.84 us  [tile_step(): pl.pallas_call(tile_kernel, out_shape=(out((2, 4, 384, 128), f32), out((6...]
    unnamed x2 -> x6, local copies, waits for them, and re-layouts: 3.54 us -> 0.02 us
    pallas_call x1 -> x2, Pallas kernels: 16.4 us -> 16.4 us  [the longest x1 15.4 us: halo(): pl.pallas_call(halo_kernel, out_shape=(jax.ShapeDtypeStruct((2, 4, 384, 1...]
where the time goes in v3:
time: 74.9 us; the launch traced here: 74.7 us
  Pallas kernels  74 us (99%)
    pallas_call x1, Pallas kernels, finish(): pl.pallas_call(finish_kernel, out_shape=(jax.ShapeDtypeStruct((2, 128, 25...  51.8 us
    pallas_call x1, Pallas kernels, halo(): pl.pallas_call(halo_kernel, out_shape=(jax.ShapeDtypeStruct((2, 4, 384, 1...  15.4 us
    pallas_call x1, Pallas kernels, tile_step(): pl.pallas_call(tile_kernel, out_shape=(out((2, 4, 384, 128), f32), out((6...  5.84 us

profile of v3, /device:TPU:1, one launch (start us, length us, event | category | flops | bytes accessed | tf_op | source)
XLA Modules:
  0.0 74.7 jit_solution(2989744763611423298)
XLA Ops:
  0.6 0.0 copy-start.1
  0.6 0.0 copy-start
  0.7 15.4 %halo.1 = (f32[2,4,384,128]{3,2,1,0:T(8,128)S(1)}, f32[128,256]{1,0:T(8,128)S(1)}, f32[2,256,256]{2,1,0:T(8,128)S(1)}, f32[2,2,256,128]{3,2,1,0:T(8,128)S(1)}) custom-call(s32[64,32]{1,0:T(8,128)} %bitcast.3, s32[16,32]{1,0:T(8,128)} %live_hbm.3, f32[2,128,256]{2,1,0:T(8,128)} %spec_ref.1, f32[2,256,256]{2,1,0:T(8,128)} %probe_hbm.1, f32[1,1,2,256,256]{4,3,2,1,0:T(8,128)} %mags.1), custom_call_target="tpu_custom_call" | custom-call | flops 400000000 | bytes 1048576 | tf_op jit(solution)/shard_map/halo/pallas_call | solution.py:172
  16.1 0.0 copy-done.1
  16.1 0.0 copy-done
  16.1 0.0 copy-start.2
  16.1 5.8 %tile_step.1 = (f32[2,4,384,128]{3,2,1,0:T(8,128)S(1)}, f32[64,3,8,128]{3,2,1,0:T(8,128)S(1)}) custom-call(s32[64,32]{1,0:T(8,128)} %bitcast.4, s32[16,32]{1,0:T(8,128)} %live_hbm.3, f32[2,4,384,128]{3,2,1,0:T(8,128)S(1)} %get-tuple-element.10.ext, f32[2,256,256]{2,1,0:T(8,128)S(1)} %get-tuple-element.11.probe.probe_ref, ...), custom_call_target="tpu_custom_call" | custom-call | flops 400000000 | bytes 1048576 | tf_op jit(solution)/shard_map/tile_step/pallas_call | solution.py:309
  22.0 0.0 copy-done.2
  22.0 51.8 %finish.1 = (f32[2,128,256]{2,1,0:T(8,128)S(1)}, f32[64,2,8,128]{3,2,1,0:T(8,128)S(1)}) custom-call(f32[64,3,8,128]{3,2,1,0:T(8,128)S(1)} %get-tuple-element.13.d_ref, f32[2,256,256]{2,1,0:T(8,128)S(1)} %get-tuple-element.11.probe.probe_ref, f32[2,4,384,128]{3,2,1,0:T(8,128)S(1)} %get-tuple-element.14.u_ref, f32[128,256]{1,0:T(8,128)S(1)} %get-tuple-element.15.den_ref, ...), custom_call_target="tpu_custom_call" | custom-call | flops 1000000000 | bytes 1048576 | tf_op jit(solution)/shard_map/finish/pallas_call | solution.py:637
  73.8 0.9 %write.1 = (f32[2,128,256]{2,1,0:T(8,128)}, f32[2,256,256]{2,1,0:T(8,128)}) custom-call(f32[2,128,256]{2,1,0:T(8,128)S(1)} %get-tuple-element.16.spec_ref, f32[64,2,8,128]{3,2,1,0:T(8,128)S(1)} %get-tuple-element.17.g_ref), custom_call_target="tpu_custom_call" | custom-call | tf_op jit(solution)/shard_map/write/pallas_call | solution.py:693
Async XLA Ops:
  0.6 15.5 %copy-start.1 = (bf16[256,256]{1,0:T(8,128)(2,1)S(1)}, bf16[256,256]{1,0:T(8,128)(2,1)}, u32[]{:S(2)}) copy-start(bf16[256,256]{1,0:T(8,128)(2,1)} %constant.5.clone.select) | copy-start | bytes 393220
  0.6 15.5 %copy-start = (bf16[2,2,2,256,256]{4,3,2,1,0:T(8,128)(2,1)S(1)}, bf16[2,2,2,256,256]{4,3,2,1,0:T(8,128)(2,1)}, u32[]{:S(2)}) copy-start(bf16[2,2,2,256,256]{4,3,2,1,0:T(8,128)(2,1)} %constant.4.clone.tables) | copy-start | bytes 3145732
  16.1 5.9 %copy-start.2 = (f32[2,128,256]{2,1,0:T(8,128)S(1)}, f32[2,128,256]{2,1,0:T(8,128)}, u32[]{:S(2)}) copy-start(f32[2,128,256]{2,1,0:T(8,128)} %spec_ref.1) | copy-start | bytes 786436

commit v4 on v3

--- a/solution.py
+++ b/solution.py
@@ -30,7 +30,12 @@
 STEP = 64
 
 
-def halo_kernel(offs_hbm, live_hbm, tile_ref, probe_hbm, mags, ext, den, probe, seen, padded, offs, live, own, fetch, cs, cr, vs, vr):
+def split(value):
+    high = value.astype(bf16)
+    return high, (value - high.astype(f32)).astype(bf16)
+
+
+def halo_kernel(offs_hbm, live_hbm, tile_ref, probe_hbm, mags, select_hbm, ext, den, probe, measured, select, padded, seen, offs, live, own, fetch, cs, cr, vs, vr):
     row = lax.axis_index("row")
     col = lax.axis_index("col")
     has = {"l": col > 0, "r": col < COLS - 1, "u": row > 0, "d": row < ROWS - 1}
@@ -42,6 +47,7 @@
     for c in small:
         c.start()
     shown = [pltpu.make_async_copy(mags.at[0, 0, s, :, pl.ds(j * 128, 128)], seen.at[s, j], fetch.at[3 + 2 * s + j]) for s in range(2) for j in range(2)]
+    shown.append(pltpu.make_async_copy(select_hbm, select, fetch.at[7]))
     barrier = pltpu.get_barrier_semaphore()
     for side in "lrud":
 
@@ -134,6 +140,13 @@
         return carry
 
     lax.fori_loop(0, 18, add, 0)
+    for c in shown:
+        c.wait()
+    for s in range(2):
+        for odd in range(2):
+            for i in range(0, 128, STEP):
+                mh, ml = split(jnp.concatenate([seen[s, j, pl.ds(odd + 2 * i, STEP, stride=2), :] for j in range(2)], 1))
+                measured[s, odd, i : i + STEP, :] = jnp.dot(mh, select[...], preferred_element_type=f32) + jnp.dot(ml, select[...], preferred_element_type=f32)
 
     for p in range(2):
         for side, part in (("l", 1), ("r", 2)):
@@ -163,22 +176,19 @@
                     up_down(p, way, part).wait_send()
                     up_down(p, back, part).wait_recv()
 
-    for c in shown:
-        c.wait()
-
-
-def halo(offs, live, tile, probe, mags):
+
+def halo(offs, live, tile, probe, mags, select):
     dma = pltpu.SemaphoreType.DMA
     return pl.pallas_call(
         halo_kernel,
-        out_shape=(jax.ShapeDtypeStruct((2, 4, 384, 128), f32), jax.ShapeDtypeStruct((128, 256), f32), jax.ShapeDtypeStruct((2, 256, 256), f32), jax.ShapeDtypeStruct((2, 2, 256, 128), f32)),
-        in_specs=[HBM] * 5,
+        out_shape=(jax.ShapeDtypeStruct((2, 4, 384, 128), f32), jax.ShapeDtypeStruct((128, 256), f32), jax.ShapeDtypeStruct((2, 256, 256), f32), jax.ShapeDtypeStruct((2, 2, 128, 256), f32)),
+        in_specs=[HBM] * 6,
         out_specs=(VMEM,) * 4,
-        scratch_shapes=[pltpu.VMEM((6, 512, 128), f32), pltpu.SMEM((ROWS * 4, COLS), jnp.int32), pltpu.SMEM((ROWS, COLS), jnp.int32), dma((2,)), dma((7,)), dma((2, 2)), dma((2, 2)), dma((2, 3, 2)), dma((2, 3, 2))],
+        scratch_shapes=[pltpu.VMEM((256, 256), bf16), pltpu.VMEM((6, 512, 128), f32), pltpu.VMEM((2, 2, 256, 128), f32), pltpu.SMEM((ROWS * 4, COLS), jnp.int32), pltpu.SMEM((ROWS, COLS), jnp.int32), dma((2,)), dma((8,)), dma((2, 2)), dma((2, 2)), dma((2, 3, 2)), dma((2, 3, 2))],
         compiler_params=pltpu.CompilerParams(collective_id=1, has_side_effects=True, vmem_limit_bytes=8 << 20),
         cost_estimate=pl.CostEstimate(flops=400000000, bytes_accessed=1 << 20, transcendentals=0),
         name="halo",
-    )(*(pltpu.with_memory_space_constraint(a, pltpu.MemorySpace.HBM) for a in (offs, live, tile, probe, mags)))
+    )(*(pltpu.with_memory_space_constraint(a, pltpu.MemorySpace.HBM) for a in (offs, live, tile, probe, mags, select)))
 
 
 def dft_tables():
@@ -198,11 +208,6 @@
     return np.stack(tables).reshape(2, 2, 2, 256, 256), select
 
 
-def split(value):
-    high = value.astype(bf16)
-    return high, (value - high.astype(f32)).astype(bf16)
-
-
 def product(a, b):
     def dot(u, v):
         return jnp.dot(u, v, preferred_element_type=f32)
@@ -210,37 +215,27 @@
     return dot(a[0], b[0]) + (dot(a[1], b[0]) + dot(a[0], b[1]))
 
 
-def tile_kernel(offs_hbm, live_hbm, ext, probe, seen, tables, select, upd, pieces, pat, wave, freq, zb, measured, offs, live, sems):
+def tile_work(offs, live, ext, probe, measured, tables, upd, pieces, pat, wave, freq, zb, placed):
     row = lax.axis_index("row")
     col = lax.axis_index("col")
+    lane = lax.broadcasted_iota(jnp.int32, (STEP, 128), 1)
 
     def table(odd, turned):
         return tables[odd, turned, 0], tables[odd, turned, 1]
 
-    fetch = [pltpu.make_async_copy(a, b, sems.at[i]) for i, (a, b) in enumerate(((offs_hbm, offs), (live_hbm, live)))]
-    for c in fetch:
-        c.start()
+    top = [offs[(row * 2 + s) * 2, col] + 128 for s in range(2)]
+    left = [offs[(row * 2 + s) * 2 + 1, col] + 128 for s in range(2)]
+    turn = [a % 128 for a in left]
+    block = [a // 128 for a in left]
+    alive = [(s < live[row, col]).astype(f32) for s in range(2)]
     for s in range(2):
-        for odd in range(2):
-            for i in range(0, 128, STEP):
-                mh, ml = split(jnp.concatenate([seen[s, j, pl.ds(odd + 2 * i, STEP, stride=2), :] for j in range(2)], 1))
-                measured[s, odd, i : i + STEP, :] = jnp.dot(mh, select[...], preferred_element_type=f32) + jnp.dot(ml, select[...], preferred_element_type=f32)
-    upd[...] = jnp.zeros_like(upd)
-    for c in fetch:
-        c.wait()
-    for s in range(2):
-        top = offs[(row * 2 + s) * 2, col] + 128
-        left = offs[(row * 2 + s) * 2 + 1, col] + 128
-        turn, block = left % 128, left // 128
-        lane = lax.broadcasted_iota(jnp.int32, (STEP, 128), 1)
-        alive = (s < live[row, col]).astype(f32)
         for i in range(0, 256, STEP):
             got = []
             for p in range(2):
-                rolled = [pltpu.roll(ext[p, jnp.minimum(block + j, 3), pl.ds(top + i, STEP), :], 128 - turn, 1) for j in range(3)]
-                halves = [jnp.where(lane < 128 - turn, rolled[j], rolled[j + 1]) for j in range(2)]
+                rolled = [pltpu.roll(ext[p, jnp.minimum(block[s] + j, 3), pl.ds(top[s] + i, STEP), :], 128 - turn[s], 1) for j in range(3)]
+                halves = [jnp.where(lane < 128 - turn[s], rolled[j], rolled[j + 1]) for j in range(2)]
                 got.append(jnp.concatenate(halves, 1))
-                pat[p, i : i + STEP, :] = got[p]
+                pat[s, p, i : i + STEP, :] = got[p]
             pr, pi = probe[0, i : i + STEP, :], probe[1, i : i + STEP, :]
             wr = pr * got[0] - pi * got[1]
             wi = pr * got[1] + pi * got[0]
@@ -251,34 +246,39 @@
                     mixed = [w[:, :128] + w[:, 128:] for w in (wr, wi)]
                 out = product(split(jnp.concatenate(mixed, 1)), table(odd, 0))
                 for p in range(2):
-                    wave[p, i : i + STEP, odd * 128 : odd * 128 + 128] = out[:, p * 128 : p * 128 + 128]
-        for odd in range(2):
+                    wave[s, p, i : i + STEP, odd * 128 : odd * 128 + 128] = out[:, p * 128 : p * 128 + 128]
+    for odd in range(2):
+        for s in range(2):
             if odd:
-                mixed = [wave[p, 0:128, :] - wave[p, 128:256, :] for p in range(2)]
+                mixed = [wave[s, p, 0:128, :] - wave[s, p, 128:256, :] for p in range(2)]
             else:
-                mixed = [wave[p, 0:128, :] + wave[p, 128:256, :] for p in range(2)]
-            freq[odd] = product(table(odd, 1), split(jnp.concatenate(mixed, 0)))
-        for odd in range(2):
+                mixed = [wave[s, p, 0:128, :] + wave[s, p, 128:256, :] for p in range(2)]
+            freq[s, odd] = product(table(odd, 1), split(jnp.concatenate(mixed, 0)))
+    for odd in range(2):
+        for s in range(2):
             for i in range(0, 128, STEP):
-                fr = freq[odd, i : i + STEP, :]
-                fi = freq[odd, 128 + i : 128 + i + STEP, :]
+                fr = freq[s, odd, i : i + STEP, :]
+                fi = freq[s, odd, 128 + i : 128 + i + STEP, :]
                 factor = measured[s, odd, i : i + STEP, :] * lax.rsqrt(jnp.maximum(fr * fr + fi * fi, 0.0625)) - 1.0
-                factor = factor * alive
+                factor = factor * alive[s]
                 for p, value in ((0, fr * factor), (1, fi * factor)):
                     high, low = split(value)
-                    zb[odd, 0, p * 128 + i : p * 128 + i + STEP, :] = high
-                    zb[odd, 1, p * 128 + i : p * 128 + i + STEP, :] = low
-        for odd in range(2):
-            freq[odd] = product(table(odd, 0), (zb[odd, 0], zb[odd, 1]))
+                    zb[s, odd, 0, p * 128 + i : p * 128 + i + STEP, :] = high
+                    zb[s, odd, 1, p * 128 + i : p * 128 + i + STEP, :] = low
+    for odd in range(2):
+        for s in range(2):
+            freq[s, odd] = product(table(odd, 0), (zb[s, odd, 0], zb[s, odd, 1]))
+    for s in range(2):
         for p in range(2):
-            e = freq[0, p * 128 : p * 128 + 128, :]
-            o = freq[1, p * 128 : p * 128 + 128, :]
-            wave[p, 0:128, :] = e + o
-            wave[p, 128:256, :] = e - o
+            e = freq[s, 0, p * 128 : p * 128 + 128, :]
+            o = freq[s, 1, p * 128 : p * 128 + 128, :]
+            wave[s, p, 0:128, :] = e + o
+            wave[s, p, 128:256, :] = e - o
+    for s in range(2):
         for i in range(0, 256, STEP):
             parts = []
             for odd in range(2):
-                mixed = [wave[p, i : i + STEP, odd * 128 : odd * 128 + 128] for p in range(2)]
+                mixed = [wave[s, p, i : i + STEP, odd * 128 : odd * 128 + 128] for p in range(2)]
                 parts.append(product(split(jnp.concatenate(mixed, 1)), table(odd, 1)))
             diff = []
             for p in range(2):
@@ -286,48 +286,30 @@
                 diff.append(jnp.concatenate([e + o, e - o], 1))
             dr, di = diff
             pr, pi = probe[0, i : i + STEP, :], probe[1, i : i + STEP, :]
-            ore, oim = pat[0, i : i + STEP, :], pat[1, i : i + STEP, :]
+            ore, oim = pat[s, 0, i : i + STEP, :], pat[s, 1, i : i + STEP, :]
             for p, grad in ((0, pr * dr + pi * di), (1, pr * di - pi * dr)):
-                first, second = (pltpu.roll(grad[:, j * 128 : j * 128 + 128], turn, 1) for j in range(2))
-                moved = (jnp.where(lane >= turn, first, 0.0), jnp.where(lane >= turn, second, first), jnp.where(lane < turn, second, 0.0))
+                first, second = (pltpu.roll(grad[:, j * 128 : j * 128 + 128], turn[s], 1) for j in range(2))
+                moved = (jnp.where(lane >= turn[s], first, 0.0), jnp.where(lane >= turn[s], second, first), jnp.where(lane < turn[s], second, 0.0))
                 for j in range(3):
-                    at = (p, jnp.minimum(block + j, 3), pl.ds(top + i, STEP))
-                    upd[at] = upd[at] + moved[j]
-            terms = (ore * dr + oim * di, ore * di - oim * dr, (ore * ore + oim * oim) * alive)
+                    placed[s, p, j, 128 + i : 128 + i + STEP, :] = moved[j]
+            terms = (ore * dr + oim * di, ore * di - oim * dr, (ore * ore + oim * oim) * alive[s])
             for lb in range(2):
                 for rb in range(STEP // 8):
                     t = lb * 32 + i // 8 + rb
                     for p in range(3):
                         value = terms[p][rb * 8 : rb * 8 + 8, lb * 128 : lb * 128 + 128]
                         pieces[t, p] = value if s == 0 else pieces[t, p] + value
-
-
-def tile_step(offs, live, ext, probe, seen):
-    tables, select = dft_tables()
-    out = jax.ShapeDtypeStruct
-    vmem = pltpu.VMEM
-    return pl.pallas_call(
-        tile_kernel,
-        out_shape=(out((2, 4, 384, 128), f32), out((64, 3, 8, 128), f32)),
-        in_specs=[HBM, HBM] + [VMEM] * 5,
-        out_specs=(VMEM,) * 2,
-        scratch_shapes=[
-            vmem((2, 256, 256), f32),
-            vmem((2, 256, 256), f32),
-            vmem((2, 256, 256), f32),
-            vmem((2, 2, 256, 256), bf16),
-            vmem((2, 2, 128, 256), f32),
-            pltpu.SMEM((ROWS * 4, COLS), jnp.int32),
-            pltpu.SMEM((ROWS, COLS), jnp.int32),
-            pltpu.SemaphoreType.DMA((2,)),
-        ],
-        compiler_params=pltpu.CompilerParams(vmem_limit_bytes=16 << 20),
-        cost_estimate=pl.CostEstimate(flops=400000000, bytes_accessed=1 << 20, transcendentals=0),
-        name="tile_step",
-    )(*(pltpu.with_memory_space_constraint(a, pltpu.MemorySpace.HBM) for a in (offs, live)), ext, probe, seen, jnp.asarray(tables), jnp.asarray(select))
-
-
-def finish_kernel(d_ref, probe_ref, u_ref, den_ref, spec_ref, spec_out, g, fv, side, fc, rp, s0, r1, s1, r2, s2, r3, wp, rw, r3w, hs, hr, es, er, ps, pr, ss1, rs1, ss2, rs2, ss3, rs3, ss4, rs4, ws, wr, zs, zr, gs, gr, know):
+    for k in range(4):
+        here = [k - block[s] for s in range(2)]
+        weight = [((a >= 0) & (a <= 2)).astype(f32) for a in here]
+        here = [jnp.clip(a, 0, 2) for a in here]
+        for p in range(2):
+            for i in range(0, 384, STEP):
+                got = [placed[s, p, here[s], pl.ds(128 + i - top[s], STEP), :] * weight[s] for s in range(2)]
+                upd[p, k, i : i + STEP, :] = got[0] + got[1]
+
+
+def finish_kernel(offs_hbm, live_hbm, ext, probe_ref, measured, tables, den_ref, spec_ref, spec_out, g, d_ref, u_ref, pat, wave, freq, zb, placed, offs, live, fetch, fv, side, fc, rp, s0, r1, s1, r2, s2, r3, wp, rw, r3w, hs, hr, es, er, ps, pr, ss1, rs1, ss2, rs2, ss3, rs3, ss4, rs4, ws, wr, zs, zr, gs, gr, know):
     row = lax.axis_index("row")
     col = lax.axis_index("col")
     core = row % 2
@@ -346,6 +328,9 @@
     has = {"l": col > 0, "r": col < COLS - 1, "u": row > 0, "d": row < ROWS - 1}
     beside = {"l": (row, col - 1), "r": (row, col + 1), "u": (row - 1, col), "d": (row + 1, col)}
 
+    small = [pltpu.make_async_copy(a, b, fetch.at[i]) for i, (a, b) in enumerate(((offs_hbm, offs), (live_hbm, live)))]
+    for c in small:
+        c.start()
     barrier = pltpu.get_barrier_semaphore()
     greet(barrier, partner)
     for axis in range(2):
@@ -382,6 +367,11 @@
         def _():
             fc[i] = jnp.zeros((2, 128, 128), f32)
 
+    placed[:, :, :, 0:128, :] = jnp.zeros((2, 2, 3, 128, 128), f32)
+    placed[:, :, :, 384:512, :] = jnp.zeros((2, 2, 3, 128, 128), f32)
+    for c in small:
+        c.wait()
+    tile_work(offs, live, ext, probe_ref, measured, tables, u_ref, d_ref, pat, wave, freq, zb, placed)
     total = d_ref[0, 2]
     for t in range(1, 64):
         total = total + d_ref[t, 2]
@@ -627,7 +617,7 @@
             lax.fori_loop(0, 15, done, 0)
 
 
-def finish(upd, pieces, den, specimen, probe_field):
+def finish(offs, live, ext, probe, measured, tables, den, specimen):
     tile = (8, 128)
     dma = pltpu.SemaphoreType.DMA
 
@@ -637,9 +627,19 @@
     return pl.pallas_call(
         finish_kernel,
         out_shape=(jax.ShapeDtypeStruct((2, 128, 256), f32), jax.ShapeDtypeStruct((64, 2, 8, 128), f32)),
-        in_specs=[VMEM] * 5,
+        in_specs=[HBM] * 2 + [VMEM] * 6,
         out_specs=(VMEM,) * 2,
         scratch_shapes=[
+            vmem(64, 3, *tile),
+            vmem(2, 4, 384, 128),
+            vmem(2, 2, 256, 256),
+            vmem(2, 2, 256, 256),
+            vmem(2, 2, 256, 256),
+            pltpu.VMEM((2, 2, 2, 256, 256), bf16),
+            vmem(2, 2, 3, 512, 128),
+            pltpu.SMEM((ROWS * 4, COLS), jnp.int32),
+            pltpu.SMEM((ROWS, COLS), jnp.int32),
+            dma((2,)),
             vmem(2, 2, 4, 128, 128),
             vmem(2, 2, 128, 128),
             vmem(2, 2, 128, 128),
@@ -675,10 +675,10 @@
             dma((2,)),
             pltpu.SemaphoreType.REGULAR((3,)),
         ],
-        compiler_params=pltpu.CompilerParams(collective_id=0, has_side_effects=True, vmem_limit_bytes=16 << 20),
+        compiler_params=pltpu.CompilerParams(collective_id=0, has_side_effects=True, vmem_limit_bytes=32 << 20),
         cost_estimate=pl.CostEstimate(flops=1000000000, bytes_accessed=1 << 20, transcendentals=0),
         name="finish",
-    )(pieces, probe_field, upd, den, specimen)
+    )(*(pltpu.with_memory_space_constraint(a, pltpu.MemorySpace.HBM) for a in (offs, live)), ext, probe, measured, tables, den, specimen)
 
 
 def write_kernel(spec_ref, g_ref, spec_out, probe_out):
@@ -702,9 +702,9 @@
 
 def shards(specimen, probe_field, scan_offsets, live_counts, magnitudes):
     offs = scan_offsets.transpose(0, 2, 3, 1).reshape(ROWS * 4, COLS)
-    ext, den, probe, seen = halo(offs, live_counts, specimen, probe_field, magnitudes)
-    upd, pieces = tile_step(offs, live_counts, ext, probe, seen)
-    return write(*finish(upd, pieces, den, specimen, probe))
+    tables, select = (jnp.asarray(a) for a in dft_tables())
+    ext, den, probe, measured = halo(offs, live_counts, specimen, probe_field, magnitudes, select)
+    return write(*finish(offs, live_counts, ext, probe, measured, tables, den, specimen))
 
 
 def solution(mesh):

time: 74.9 us -> 71.4 us (0.953)
  Pallas kernels: 74 us -> 70.4 us
    pallas_call x1 -> x0, Pallas kernels: 5.84 us -> none  [tile_step(): pl.pallas_call(tile_kernel, out_shape=(out((2, 4, 384, 128), f32), out((6...]
    pallas_call x1, Pallas kernels: 51.8 us -> 54 us  [finish(): pl.pallas_call(finish_kernel, out_shape=(jax.ShapeDtypeStruct((2, 128, 25...]
where the time goes in v4:
time: 71.4 us; the launch traced here: 71.1 us
  Pallas kernels  70.4 us (99%)
    pallas_call x1, Pallas kernels, finish(): pl.pallas_call(finish_kernel, out_shape=(jax.ShapeDtypeStruct((2, 128, 25...  54 us
    pallas_call x1, Pallas kernels, halo(): pl.pallas_call(halo_kernel, out_shape=(jax.ShapeDtypeStruct((2, 4, 384, 1...  15.4 us

profile of v4, /device:TPU:1, one launch (start us, length us, event | category | flops | bytes accessed | tf_op | source)
XLA Modules:
  0.0 71.1 jit_solution(6073546343463253240)
XLA Ops:
  0.6 0.0 copy-start.1
  0.6 0.0 copy-start
  0.7 15.4 %halo.1 = (f32[2,4,384,128]{3,2,1,0:T(8,128)S(1)}, f32[128,256]{1,0:T(8,128)S(1)}, f32[2,256,256]{2,1,0:T(8,128)S(1)}, f32[2,2,128,256]{3,2,1,0:T(8,128)S(1)}) custom-call(s32[64,32]{1,0:T(8,128)} %bitcast.3, s32[16,32]{1,0:T(8,128)} %live_hbm.3, f32[2,128,256]{2,1,0:T(8,128)} %spec_ref.1, f32[2,256,256]{2,1,0:T(8,128)} %probe_hbm.1, ...), custom_call_target="tpu_custom_call" | custom-call | flops 400000000 | bytes 1048576 | tf_op jit(solution)/shard_map/halo/pallas_call | solution.py:182
  16.1 0.0 copy-done.1
  16.1 0.0 copy-done
  16.1 54.0 %finish.1 = (f32[2,128,256]{2,1,0:T(8,128)S(1)}, f32[64,2,8,128]{3,2,1,0:T(8,128)S(1)}) custom-call(s32[64,32]{1,0:T(8,128)} %bitcast.4, s32[16,32]{1,0:T(8,128)} %live_hbm.3, f32[2,4,384,128]{3,2,1,0:T(8,128)S(1)} %get-tuple-element.8.ext, f32[2,256,256]{2,1,0:T(8,128)S(1)} %get-tuple-element.9.probe_ref, ...), custom_call_target="tpu_custom_call" | custom-call | flops 1000000000 | bytes 1048576 | tf_op jit(solution)/shard_map/finish/pallas_call | solution.py:627
  70.2 0.9 %write.1 = (f32[2,128,256]{2,1,0:T(8,128)}, f32[2,256,256]{2,1,0:T(8,128)}) custom-call(f32[2,128,256]{2,1,0:T(8,128)S(1)} %get-tuple-element.12.spec_ref, f32[64,2,8,128]{3,2,1,0:T(8,128)S(1)} %get-tuple-element.13.g_ref), custom_call_target="tpu_custom_call" | custom-call | tf_op jit(solution)/shard_map/write/pallas_call | solution.py:693
Async XLA Ops:
  0.6 15.5 %copy-start.1 = (bf16[2,2,2,256,256]{4,3,2,1,0:T(8,128)(2,1)S(1)}, bf16[2,2,2,256,256]{4,3,2,1,0:T(8,128)(2,1)}, u32[]{:S(2)}) copy-start(bf16[2,2,2,256,256]{4,3,2,1,0:T(8,128)(2,1)} %constant.4.clone.tables) | copy-start | bytes 3145732
  0.6 15.5 %copy-start = (f32[2,128,256]{2,1,0:T(8,128)S(1)}, f32[2,128,256]{2,1,0:T(8,128)}, u32[]{:S(2)}) copy-start(f32[2,128,256]{2,1,0:T(8,128)} %spec_ref.1) | copy-start | bytes 786436

commit v5 on v4

--- a/solution.py
+++ b/solution.py
@@ -340,12 +340,9 @@
     def along(d):
         return device(core, x, y, (z + d) % 16)
 
-    greet(barrier, along(1))
-    greet(barrier, along(15))
-
-    def tell(n, d):
-        for way in (d, 16 - d):
-            pl.semaphore_signal(know.at[n], inc=1, device_id=along(way), device_id_type=MESH)
+    for d in range(1, 5):
+        greet(barrier, along(d))
+        greet(barrier, along(16 - d))
 
     for way in "lrud":
 
@@ -353,7 +350,7 @@
         def _():
             greet(barrier, beside[way])
 
-    expected = 9 + sum(has[way].astype(jnp.int32) for way in "lrud")
+    expected = 15 + sum(has[way].astype(jnp.int32) for way in "lrud")
 
     for i, way in enumerate("ud"):
 
@@ -377,7 +374,8 @@
         total = total + d_ref[t, 2]
     wp[0] = total
     pl.semaphore_wait(barrier, expected)
-    tell(0, 1)
+    for d in (4, 12):
+        pl.semaphore_signal(know, inc=1, device_id=along(d), device_id_type=MESH)
 
     def vertical(p, part, way, inward=False):
         at = (0, 3, pl.ds(1, 2))[part]
@@ -410,8 +408,6 @@
         if d == 2:
             first = go(remote(wp.at[0], rw.at[0], ws.at[0], wr.at[0], partner))
 
-    pl.semaphore_wait(know.at[0], 2)
-    tell(1, 2)
 
     def join(color, d):
         pairs[color, d].wait_recv()
@@ -422,8 +418,6 @@
     for d in near:
         for color in range(2):
             join(color, d)
-    pl.semaphore_wait(know.at[1], 2)
-    tell(2, 4)
     one = {}
     for e in near + (0,):
         for d in near:
@@ -461,10 +455,10 @@
     for c in waves:
         c.wait_recv()
     wp[3] = wp[2] + (rw[4] + (rw[5] + rw[6]))
-    pl.semaphore_wait(know.at[2], 2)
+    pl.semaphore_wait(know, 2)
 
     def root(color):
-        return 2 + 8 * color + 4 * core
+        return 4 * color + 2 * core
 
     def slot(color):
         return base + color * 16 + jnp.where(color == 0, x * 4 + y, y * 4 + x)
@@ -473,23 +467,25 @@
         for e in near:
             two[color, e].wait_recv()
         s2[color] = s1[color, 0] + (r2[color, 0] + (r2[color, 1] + r2[color, 2]))
-        goal = root(color)
-
-        @pl.when(z != goal)
+        for n in range(2):
+            goal = root(color) + 8 * n
+
+            @pl.when(z != goal)
+            def _():
+                remote(s2.at[color], r3.at[z], zs.at[color, n, 0], zr.at[0], device(core, x, y, goal)).start()
+                remote(wp.at[3], r3w.at[z], zs.at[color, n, 1], zr.at[1], device(core, x, y, goal)).start()
+
+    for color in range(2):
+
+        @pl.when(z % 8 == root(color))
         def _():
-            at = (z - goal + 16) % 16
-            remote(s2.at[color], r3.at[at - 1], zs.at[color, 0], zr.at[0], device(core, x, y, goal)).start()
-            remote(wp.at[3], r3w.at[at - 1], zs.at[color, 1], zr.at[1], device(core, x, y, goal)).start()
-
-    for color in range(2):
-
-        @pl.when(z == root(color))
-        def _():
-            pltpu.make_async_copy(r3, r3, zr.at[0]).wait()
-            pltpu.make_async_copy(r3w, r3w, zr.at[1]).wait()
-            full = s2[color]
-            weight = wp[3]
-            for i in range(15):
+            r3[z] = s2[color]
+            r3w[z] = wp[3]
+            pltpu.make_async_copy(r3.at[pl.ds(0, 15)], r3.at[pl.ds(0, 15)], zr.at[0]).wait()
+            pltpu.make_async_copy(r3w.at[pl.ds(0, 15)], r3w.at[pl.ds(0, 15)], zr.at[1]).wait()
+            full = r3[0]
+            weight = r3w[0]
+            for i in range(1, 16):
                 full = full + r3[i]
                 weight = weight + r3w[i]
             mean = jnp.sum(weight) * (1.0 / 65536.0)
@@ -499,12 +495,8 @@
             lanes = pl.ds(pl.multiple_of((t // 32) * 128, 128), 128)
             for p in range(2):
                 g[t, p] = probe_ref[p, rows, lanes] + full[p] / scale
-
-            def send(i, carry):
-                remote(g.at[t], g.at[t], gs.at[i - 1], gr.at[color], device(core, x, y, (z + i) % 16)).start()
-                return carry
-
-            lax.fori_loop(1, 16, send, 0)
+            for i in (4, 3, 13, 2, 14, 1, 15):
+                remote(g.at[t], g.at[t], gs.at[i % 8], gr.at[color], along(i)).start()
 
     for i, (way, at) in enumerate((("l", 0), ("r", 3))):
         for p in range(2):
@@ -520,8 +512,8 @@
                 lateral(p, way).start()
 
     def away(color):
-        d = (z - root(color) + 16) % 16
-        return jnp.minimum(d, 16 - d)
+        d = (z - root(color) + 16) % 8
+        return jnp.minimum(d, 8 - d)
 
     nearer = (away(1) < away(0)).astype(jnp.int32)
     colors = (nearer, 1 - nearer)
@@ -540,7 +532,7 @@
     for n, color in enumerate(colors):
         t = slot(color)
 
-        @pl.when(z != root(color))
+        @pl.when(z % 8 != root(color))
         def _():
             pltpu.make_async_copy(g.at[t], g.at[t], gr.at[color]).wait()
 
@@ -601,20 +593,18 @@
 
     for color in range(2):
 
-        @pl.when(z != root(color))
-        def _():
-            pltpu.make_async_copy(s2.at[color], s2.at[color], zs.at[color, 0]).wait()
-            pltpu.make_async_copy(wp.at[3], wp.at[3], zs.at[color, 1]).wait()
-
-        @pl.when(z == root(color))
+        for n in range(2):
+
+            @pl.when(z != root(color) + 8 * n)
+            def _():
+                pltpu.make_async_copy(s2.at[color], s2.at[color], zs.at[color, n, 0]).wait()
+                pltpu.make_async_copy(wp.at[3], wp.at[3], zs.at[color, n, 1]).wait()
+
+        @pl.when(z % 8 == root(color))
         def _():
             t = slot(color)
-
-            def done(i, carry):
+            for i in (4, 3, 5, 2, 6, 1, 7):
                 pltpu.make_async_copy(g.at[t], g.at[t], gs.at[i]).wait()
-                return carry
-
-            lax.fori_loop(0, 15, done, 0)
 
 
 def finish(offs, live, ext, probe, measured, tables, den, specimen):
@@ -649,10 +639,10 @@
             vmem(2, 4, 3, *tile),
             vmem(2, 3, 3, *tile),
             vmem(2, 3, *tile),
-            vmem(15, 3, *tile),
+            vmem(16, 3, *tile),
             vmem(4, *tile),
             vmem(7, *tile),
-            vmem(15, *tile),
+            vmem(16, *tile),
             dma((2, 3, 2)),
             dma((2, 3, 2)),
             dma((2, 2)),
@@ -669,11 +659,11 @@
             dma((2, 3, 4)),
             dma((7,)),
             dma((7,)),
-            dma((2, 2)),
+            dma((2, 2, 2)),
             dma((2,)),
-            dma((15,)),
+            dma((8,)),
             dma((2,)),
-            pltpu.SemaphoreType.REGULAR((3,)),
+            pltpu.SemaphoreType.REGULAR,
         ],
         compiler_params=pltpu.CompilerParams(collective_id=0, has_side_effects=True, vmem_limit_bytes=32 << 20),
         cost_estimate=pl.CostEstimate(flops=1000000000, bytes_accessed=1 << 20, transcendentals=0),

time: 71.4 us -> 68.2 us (0.955)
  Pallas kernels: 70.4 us -> 67.3 us
    pallas_call x1, Pallas kernels: 54 us -> 50.9 us  [finish(): pl.pallas_call(finish_kernel, out_shape=(jax.ShapeDtypeStruct((2, 128, 25...]
where the time goes in v5:
time: 68.2 us; the launch traced here: 68 us
  Pallas kernels  67.3 us (99%)
    pallas_call x1, Pallas kernels, finish(): pl.pallas_call(finish_kernel, out_shape=(jax.ShapeDtypeStruct((2, 128, 25...  50.9 us
    pallas_call x1, Pallas kernels, halo(): pl.pallas_call(halo_kernel, out_shape=(jax.ShapeDtypeStruct((2, 4, 384, 1...  15.4 us

profile of v5, /device:TPU:1, one launch (start us, length us, event | category | flops | bytes accessed | tf_op | source)
XLA Modules:
  0.0 68.0 jit_solution(2054590015302784954)
XLA Ops:
  0.6 0.0 copy-start.1
  0.6 0.0 copy-start
  0.7 15.4 %halo.1 = (f32[2,4,384,128]{3,2,1,0:T(8,128)S(1)}, f32[128,256]{1,0:T(8,128)S(1)}, f32[2,256,256]{2,1,0:T(8,128)S(1)}, f32[2,2,128,256]{3,2,1,0:T(8,128)S(1)}) custom-call(s32[64,32]{1,0:T(8,128)} %bitcast.3, s32[16,32]{1,0:T(8,128)} %live_hbm.3, f32[2,128,256]{2,1,0:T(8,128)} %spec_ref.1, f32[2,256,256]{2,1,0:T(8,128)} %probe_hbm.1, ...), custom_call_target="tpu_custom_call" | custom-call | flops 400000000 | bytes 1048576 | tf_op jit(solution)/shard_map/halo/pallas_call | solution.py:182
  16.1 0.0 copy-done.1
  16.1 0.0 copy-done
  16.1 50.9 %finish.1 = (f32[2,128,256]{2,1,0:T(8,128)S(1)}, f32[64,2,8,128]{3,2,1,0:T(8,128)S(1)}) custom-call(s32[64,32]{1,0:T(8,128)} %bitcast.4, s32[16,32]{1,0:T(8,128)} %live_hbm.3, f32[2,4,384,128]{3,2,1,0:T(8,128)S(1)} %get-tuple-element.8.ext, f32[2,256,256]{2,1,0:T(8,128)S(1)} %get-tuple-element.9.probe_ref, ...), custom_call_target="tpu_custom_call" | custom-call | flops 1000000000 | bytes 1048576 | tf_op jit(solution)/shard_map/finish/pallas_call | solution.py:617
  67.1 0.9 %write.1 = (f32[2,128,256]{2,1,0:T(8,128)}, f32[2,256,256]{2,1,0:T(8,128)}) custom-call(f32[2,128,256]{2,1,0:T(8,128)S(1)} %get-tuple-element.12.spec_ref, f32[64,2,8,128]{3,2,1,0:T(8,128)S(1)} %get-tuple-element.13.g_ref), custom_call_target="tpu_custom_call" | custom-call | tf_op jit(solution)/shard_map/write/pallas_call | solution.py:683
Async XLA Ops:
  0.6 15.5 %copy-start.1 = (bf16[2,2,2,256,256]{4,3,2,1,0:T(8,128)(2,1)S(1)}, bf16[2,2,2,256,256]{4,3,2,1,0:T(8,128)(2,1)}, u32[]{:S(2)}) copy-start(bf16[2,2,2,256,256]{4,3,2,1,0:T(8,128)(2,1)} %constant.4.clone.tables) | copy-start | bytes 3145732
  0.6 15.5 %copy-start = (f32[2,128,256]{2,1,0:T(8,128)S(1)}, f32[2,128,256]{2,1,0:T(8,128)}, u32[]{:S(2)}) copy-start(f32[2,128,256]{2,1,0:T(8,128)} %spec_ref.1) | copy-start | bytes 786436

commit v6 on v5

--- a/solution.py
+++ b/solution.py
@@ -140,6 +140,18 @@
         return carry
 
     lax.fori_loop(0, 18, add, 0)
+    for p in range(2):
+        for side, part in (("l", 1), ("r", 2)):
+
+            @pl.when(has[side])
+            def _():
+                across(p, "r" if side == "l" else "l").wait_recv()
+                for way in "ud":
+
+                    @pl.when(has[way])
+                    def _():
+                        up_down(p, way, part).start()
+
     for c in shown:
         c.wait()
     for s in range(2):
@@ -147,18 +159,6 @@
             for i in range(0, 128, STEP):
                 mh, ml = split(jnp.concatenate([seen[s, j, pl.ds(odd + 2 * i, STEP, stride=2), :] for j in range(2)], 1))
                 measured[s, odd, i : i + STEP, :] = jnp.dot(mh, select[...], preferred_element_type=f32) + jnp.dot(ml, select[...], preferred_element_type=f32)
-
-    for p in range(2):
-        for side, part in (("l", 1), ("r", 2)):
-
-            @pl.when(has[side])
-            def _():
-                across(p, "r" if side == "l" else "l").wait_recv()
-                for way in "ud":
-
-                    @pl.when(has[way])
-                    def _():
-                        up_down(p, way, part).start()
 
     for p in range(2):
         for side in "lr":
@@ -244,9 +244,13 @@
                     mixed = [w[:, :128] - w[:, 128:] for w in (wr, wi)]
                 else:
                     mixed = [w[:, :128] + w[:, 128:] for w in (wr, wi)]
-                out = product(split(jnp.concatenate(mixed, 1)), table(odd, 0))
-                for p in range(2):
-                    wave[s, p, i : i + STEP, odd * 128 : odd * 128 + 128] = out[:, p * 128 : p * 128 + 128]
+                high, low = split(jnp.concatenate(mixed, 1))
+                zb[s, odd, 0, i : i + STEP, :] = high
+                zb[s, odd, 1, i : i + STEP, :] = low
+        for odd in range(2):
+            out = product((zb[s, odd, 0], zb[s, odd, 1]), table(odd, 0))
+            for p in range(2):
+                wave[s, p, :, odd * 128 : odd * 128 + 128] = out[:, p * 128 : p * 128 + 128]
     for odd in range(2):
         for s in range(2):
             if odd:
@@ -275,14 +279,17 @@
             wave[s, p, 0:128, :] = e + o
             wave[s, p, 128:256, :] = e - o
     for s in range(2):
+        for odd in range(2):
+            for i in range(0, 256, STEP):
+                high, low = split(jnp.concatenate([wave[s, p, i : i + STEP, odd * 128 : odd * 128 + 128] for p in range(2)], 1))
+                zb[s, odd, 0, i : i + STEP, :] = high
+                zb[s, odd, 1, i : i + STEP, :] = low
+            freq[s, odd] = product((zb[s, odd, 0], zb[s, odd, 1]), table(odd, 1))
+    for s in range(2):
         for i in range(0, 256, STEP):
-            parts = []
-            for odd in range(2):
-                mixed = [wave[s, p, i : i + STEP, odd * 128 : odd * 128 + 128] for p in range(2)]
-                parts.append(product(split(jnp.concatenate(mixed, 1)), table(odd, 1)))
             diff = []
             for p in range(2):
-                e, o = (parts[odd][:, p * 128 : p * 128 + 128] for odd in range(2))
+                e, o = (freq[s, odd, i : i + STEP, p * 128 : p * 128 + 128] for odd in range(2))
                 diff.append(jnp.concatenate([e + o, e - o], 1))
             dr, di = diff
             pr, pi = probe[0, i : i + STEP, :], probe[1, i : i + STEP, :]

time: 68.2 us -> 67.8 us (level)
  no operation moved by 1% of the time
where the time goes in v6:
time: 67.8 us; the launch traced here: 67.5 us
  Pallas kernels  66.8 us (99%)
  between operations  0.68 us (1%)
    pallas_call x1, Pallas kernels, finish(): pl.pallas_call(finish_kernel, out_shape=(jax.ShapeDtypeStruct((2, 128, 25...  50.5 us
    pallas_call x1, Pallas kernels, halo(): pl.pallas_call(halo_kernel, out_shape=(jax.ShapeDtypeStruct((2, 4, 384, 1...  15.4 us

profile of v6, /device:TPU:1, one launch (start us, length us, event | category | flops | bytes accessed | tf_op | source)
XLA Modules:
  0.0 67.5 jit_solution(1856232272789952075)
XLA Ops:
  0.6 0.0 copy-start.1
  0.6 0.0 copy-start
  0.7 15.4 %halo.1 = (f32[2,4,384,128]{3,2,1,0:T(8,128)S(1)}, f32[128,256]{1,0:T(8,128)S(1)}, f32[2,256,256]{2,1,0:T(8,128)S(1)}, f32[2,2,128,256]{3,2,1,0:T(8,128)S(1)}) custom-call(s32[64,32]{1,0:T(8,128)} %bitcast.3, s32[16,32]{1,0:T(8,128)} %live_hbm.3, f32[2,128,256]{2,1,0:T(8,128)} %spec_ref.1, f32[2,256,256]{2,1,0:T(8,128)} %probe_hbm.1, ...), custom_call_target="tpu_custom_call" | custom-call | flops 400000000 | bytes 1048576 | tf_op jit(solution)/shard_map/halo/pallas_call | solution.py:182
  16.1 0.0 copy-done.1
  16.1 0.0 copy-done
  16.1 50.5 %finish.1 = (f32[2,128,256]{2,1,0:T(8,128)S(1)}, f32[64,2,8,128]{3,2,1,0:T(8,128)S(1)}) custom-call(s32[64,32]{1,0:T(8,128)} %bitcast.4, s32[16,32]{1,0:T(8,128)} %live_hbm.3, f32[2,4,384,128]{3,2,1,0:T(8,128)S(1)} %get-tuple-element.8.ext, f32[2,256,256]{2,1,0:T(8,128)S(1)} %get-tuple-element.9.probe_ref, ...), custom_call_target="tpu_custom_call" | custom-call | flops 1000000000 | bytes 1048576 | tf_op jit(solution)/shard_map/finish/pallas_call | solution.py:624
  66.6 0.9 %write.1 = (f32[2,128,256]{2,1,0:T(8,128)}, f32[2,256,256]{2,1,0:T(8,128)}) custom-call(f32[2,128,256]{2,1,0:T(8,128)S(1)} %get-tuple-element.12.spec_ref, f32[64,2,8,128]{3,2,1,0:T(8,128)S(1)} %get-tuple-element.13.g_ref), custom_call_target="tpu_custom_call" | custom-call | tf_op jit(solution)/shard_map/write/pallas_call | solution.py:690
Async XLA Ops:
  0.6 15.5 %copy-start.1 = (bf16[2,2,2,256,256]{4,3,2,1,0:T(8,128)(2,1)S(1)}, bf16[2,2,2,256,256]{4,3,2,1,0:T(8,128)(2,1)}, u32[]{:S(2)}) copy-start(bf16[2,2,2,256,256]{4,3,2,1,0:T(8,128)(2,1)} %constant.4.clone.tables) | copy-start | bytes 3145732
  0.6 15.5 %copy-start = (f32[2,128,256]{2,1,0:T(8,128)S(1)}, f32[2,128,256]{2,1,0:T(8,128)}, u32[]{:S(2)}) copy-start(f32[2,128,256]{2,1,0:T(8,128)} %spec_ref.1) | copy-start | bytes 786436

commit v7 on v6

--- a/solution.py
+++ b/solution.py
@@ -35,7 +35,7 @@
     return high, (value - high.astype(f32)).astype(bf16)
 
 
-def halo_kernel(offs_hbm, live_hbm, tile_ref, probe_hbm, mags, select_hbm, ext, den, probe, measured, select, padded, seen, offs, live, own, fetch, cs, cr, vs, vr):
+def halo_kernel(offs_hbm, live_hbm, tile_ref, probe_hbm, mags, select_hbm, pat, den, probe, measured, ext, select, padded, seen, offs, live, own, fetch, cs, cr, vs, vr):
     row = lax.axis_index("row")
     col = lax.axis_index("col")
     has = {"l": col > 0, "r": col < COLS - 1, "u": row > 0, "d": row < ROWS - 1}
@@ -125,7 +125,7 @@
         inside = (a >= 0) & (a < ROWS) & (b >= 0) & (b < COLS)
         a = jnp.clip(a, 0, ROWS - 1)
         b = jnp.clip(b, 0, COLS - 1)
-        down = da * 128 + offs[(a * 2 + s) * 2, b]
+        down = da * 128 + jnp.clip(offs[(a * 2 + s) * 2, b], -128, 0)
         across = db * 256 + offs[(a * 2 + s) * 2 + 1, b]
         on = (inside & (s < live[a, b]) & (across > -256) & (across < 256)).astype(f32)
         across = jnp.clip(across, -256, 255)
@@ -176,15 +176,26 @@
                     up_down(p, way, part).wait_send()
                     up_down(p, back, part).wait_recv()
 
+    lane = lax.broadcasted_iota(jnp.int32, (STEP, 128), 1)
+    for s in range(2):
+        top = jnp.clip(offs[(row * 2 + s) * 2, col] + 128, 0, 128)
+        left = jnp.clip(offs[(row * 2 + s) * 2 + 1, col] + 128, 0, 256)
+        turn, block = left % 128, left // 128
+        for i in range(0, 256, STEP):
+            for p in range(2):
+                rolled = [pltpu.roll(ext[p, jnp.minimum(block + j, 3), pl.ds(top + i, STEP), :], 128 - turn, 1) for j in range(3)]
+                for j in range(2):
+                    pat[s, p, i : i + STEP, j * 128 : j * 128 + 128] = jnp.where(lane < 128 - turn, rolled[j], rolled[j + 1])
+
 
 def halo(offs, live, tile, probe, mags, select):
     dma = pltpu.SemaphoreType.DMA
     return pl.pallas_call(
         halo_kernel,
-        out_shape=(jax.ShapeDtypeStruct((2, 4, 384, 128), f32), jax.ShapeDtypeStruct((128, 256), f32), jax.ShapeDtypeStruct((2, 256, 256), f32), jax.ShapeDtypeStruct((2, 2, 128, 256), f32)),
+        out_shape=(jax.ShapeDtypeStruct((2, 2, 256, 256), f32), jax.ShapeDtypeStruct((128, 256), f32), jax.ShapeDtypeStruct((2, 256, 256), f32), jax.ShapeDtypeStruct((2, 2, 128, 256), f32)),
         in_specs=[HBM] * 6,
         out_specs=(VMEM,) * 4,
-        scratch_shapes=[pltpu.VMEM((256, 256), bf16), pltpu.VMEM((6, 512, 128), f32), pltpu.VMEM((2, 2, 256, 128), f32), pltpu.SMEM((ROWS * 4, COLS), jnp.int32), pltpu.SMEM((ROWS, COLS), jnp.int32), dma((2,)), dma((8,)), dma((2, 2)), dma((2, 2)), dma((2, 3, 2)), dma((2, 3, 2))],
+        scratch_shapes=[pltpu.VMEM((2, 4, 384, 128), f32), pltpu.VMEM((256, 256), bf16), pltpu.VMEM((6, 512, 128), f32), pltpu.VMEM((2, 2, 256, 128), f32), pltpu.SMEM((ROWS * 4, COLS), jnp.int32), pltpu.SMEM((ROWS, COLS), jnp.int32), dma((2,)), dma((8,)), dma((2, 2)), dma((2, 2)), dma((2, 3, 2)), dma((2, 3, 2))],
         compiler_params=pltpu.CompilerParams(collective_id=1, has_side_effects=True, vmem_limit_bytes=8 << 20),
         cost_estimate=pl.CostEstimate(flops=400000000, bytes_accessed=1 << 20, transcendentals=0),
         name="halo",
@@ -215,7 +226,7 @@
     return dot(a[0], b[0]) + (dot(a[1], b[0]) + dot(a[0], b[1]))
 
 
-def tile_work(offs, live, ext, probe, measured, tables, upd, pieces, pat, wave, freq, zb, placed):
+def tile_work(small, offs, live, probe, measured, tables, upd, pieces, pat, wave, freq, zb, placed):
     row = lax.axis_index("row")
     col = lax.axis_index("col")
     lane = lax.broadcasted_iota(jnp.int32, (STEP, 128), 1)
@@ -223,19 +234,9 @@
     def table(odd, turned):
         return tables[odd, turned, 0], tables[odd, turned, 1]
 
-    top = [offs[(row * 2 + s) * 2, col] + 128 for s in range(2)]
-    left = [offs[(row * 2 + s) * 2 + 1, col] + 128 for s in range(2)]
-    turn = [a % 128 for a in left]
-    block = [a // 128 for a in left]
-    alive = [(s < live[row, col]).astype(f32) for s in range(2)]
     for s in range(2):
         for i in range(0, 256, STEP):
-            got = []
-            for p in range(2):
-                rolled = [pltpu.roll(ext[p, jnp.minimum(block[s] + j, 3), pl.ds(top[s] + i, STEP), :], 128 - turn[s], 1) for j in range(3)]
-                halves = [jnp.where(lane < 128 - turn[s], rolled[j], rolled[j + 1]) for j in range(2)]
-                got.append(jnp.concatenate(halves, 1))
-                pat[s, p, i : i + STEP, :] = got[p]
+            got = [pat[s, p, i : i + STEP, :] for p in range(2)]
             pr, pi = probe[0, i : i + STEP, :], probe[1, i : i + STEP, :]
             wr = pr * got[0] - pi * got[1]
             wi = pr * got[1] + pi * got[0]
@@ -258,6 +259,13 @@
             else:
                 mixed = [wave[s, p, 0:128, :] + wave[s, p, 128:256, :] for p in range(2)]
             freq[s, odd] = product(table(odd, 1), split(jnp.concatenate(mixed, 0)))
+    for c in small:
+        c.wait()
+    top = [jnp.clip(offs[(row * 2 + s) * 2, col] + 128, 0, 128) for s in range(2)]
+    left = [jnp.clip(offs[(row * 2 + s) * 2 + 1, col] + 128, 0, 256) for s in range(2)]
+    turn = [a % 128 for a in left]
+    block = [a // 128 for a in left]
+    alive = [(s < live[row, col]).astype(f32) for s in range(2)]
     for odd in range(2):
         for s in range(2):
             for i in range(0, 128, STEP):
@@ -316,7 +324,7 @@
                 upd[p, k, i : i + STEP, :] = got[0] + got[1]
 
 
-def finish_kernel(offs_hbm, live_hbm, ext, probe_ref, measured, tables, den_ref, spec_ref, spec_out, g, d_ref, u_ref, pat, wave, freq, zb, placed, offs, live, fetch, fv, side, fc, rp, s0, r1, s1, r2, s2, r3, wp, rw, r3w, hs, hr, es, er, ps, pr, ss1, rs1, ss2, rs2, ss3, rs3, ss4, rs4, ws, wr, zs, zr, gs, gr, know):
+def finish_kernel(offs_hbm, live_hbm, pat, probe_ref, measured, tables, den_ref, spec_ref, spec_out, g, d_ref, u_ref, wave, freq, zb, placed, offs, live, fetch, fv, side, fc, rp, s0, r1, s1, r2, s2, r3, wp, rw, r3w, hs, hr, es, er, ps, pr, ss1, rs1, ss2, rs2, ss3, rs3, ss4, rs4, ws, wr, zs, zr, gs, gr, know):
     row = lax.axis_index("row")
     col = lax.axis_index("col")
     core = row % 2
@@ -373,9 +381,7 @@
 
     placed[:, :, :, 0:128, :] = jnp.zeros((2, 2, 3, 128, 128), f32)
     placed[:, :, :, 384:512, :] = jnp.zeros((2, 2, 3, 128, 128), f32)
-    for c in small:
-        c.wait()
-    tile_work(offs, live, ext, probe_ref, measured, tables, u_ref, d_ref, pat, wave, freq, zb, placed)
+    tile_work(small, offs, live, probe_ref, measured, tables, u_ref, d_ref, pat, wave, freq, zb, placed)
     total = d_ref[0, 2]
     for t in range(1, 64):
         total = total + d_ref[t, 2]
@@ -614,7 +620,7 @@
                 pltpu.make_async_copy(g.at[t], g.at[t], gs.at[i]).wait()
 
 
-def finish(offs, live, ext, probe, measured, tables, den, specimen):
+def finish(offs, live, pat, probe, measured, tables, den, specimen):
     tile = (8, 128)
     dma = pltpu.SemaphoreType.DMA
 
@@ -629,7 +635,6 @@
         scratch_shapes=[
             vmem(64, 3, *tile),
             vmem(2, 4, 384, 128),
-            vmem(2, 2, 256, 256),
             vmem(2, 2, 256, 256),
             vmem(2, 2, 256, 256),
             pltpu.VMEM((2, 2, 2, 256, 256), bf16),
@@ -675,7 +680,7 @@
         compiler_params=pltpu.CompilerParams(collective_id=0, has_side_effects=True, vmem_limit_bytes=32 << 20),
         cost_estimate=pl.CostEstimate(flops=1000000000, bytes_accessed=1 << 20, transcendentals=0),
         name="finish",
-    )(*(pltpu.with_memory_space_constraint(a, pltpu.MemorySpace.HBM) for a in (offs, live)), ext, probe, measured, tables, den, specimen)
+    )(*(pltpu.with_memory_space_constraint(a, pltpu.MemorySpace.HBM) for a in (offs, live)), pat, probe, measured, tables, den, specimen)
 
 
 def write_kernel(spec_ref, g_ref, spec_out, probe_out):
@@ -700,8 +705,8 @@
 def shards(specimen, probe_field, scan_offsets, live_counts, magnitudes):
     offs = scan_offsets.transpose(0, 2, 3, 1).reshape(ROWS * 4, COLS)
     tables, select = (jnp.asarray(a) for a in dft_tables())
-    ext, den, probe, measured = halo(offs, live_counts, specimen, probe_field, magnitudes, select)
-    return write(*finish(offs, live_counts, ext, probe, measured, tables, den, specimen))
+    pat, den, probe, measured = halo(offs, live_counts, specimen, probe_field, magnitudes, select)
+    return write(*finish(offs, live_counts, pat, probe, measured, tables, den, specimen))
 
 
 def solution(mesh):

time: 67.8 us -> 68.2 us (level)
  no operation moved by 1% of the time
where the time goes in v7:
time: 68.2 us; the launch traced here: 68 us
  Pallas kernels  67.3 us (99%)
    pallas_call x1, Pallas kernels, finish(): pl.pallas_call(finish_kernel, out_shape=(jax.ShapeDtypeStruct((2, 128, 25...  50.5 us
    pallas_call x1, Pallas kernels, halo(): pl.pallas_call(halo_kernel, out_shape=(jax.ShapeDtypeStruct((2, 2, 256, 2...  15.9 us

profile of v7, /device:TPU:1, one launch (start us, length us, event | category | flops | bytes accessed | tf_op | source)
XLA Modules:
  0.0 68.0 jit_solution(2591637250963876034)
XLA Ops:
  0.6 0.0 copy-start.1
  0.6 0.0 copy-start
  0.7 15.9 %halo.1 = (f32[2,2,256,256]{3,2,1,0:T(8,128)S(1)}, f32[128,256]{1,0:T(8,128)S(1)}, f32[2,256,256]{2,1,0:T(8,128)S(1)}, f32[2,2,128,256]{3,2,1,0:T(8,128)S(1)}) custom-call(s32[64,32]{1,0:T(8,128)} %bitcast.3, s32[16,32]{1,0:T(8,128)} %live_hbm.3, f32[2,128,256]{2,1,0:T(8,128)} %spec_ref.1, f32[2,256,256]{2,1,0:T(8,128)} %probe_hbm.1, ...), custom_call_target="tpu_custom_call" | custom-call | flops 400000000 | bytes 1048576 | tf_op jit(solution)/shard_map/halo/pallas_call | solution.py:193
  16.6 0.0 copy-done.1
  16.6 0.0 copy-done
  16.6 50.5 %finish.1 = (f32[2,128,256]{2,1,0:T(8,128)S(1)}, f32[64,2,8,128]{3,2,1,0:T(8,128)S(1)}) custom-call(s32[64,32]{1,0:T(8,128)} %bitcast.4, s32[16,32]{1,0:T(8,128)} %live_hbm.3, f32[2,2,256,256]{3,2,1,0:T(8,128)S(1)} %get-tuple-element.8.pat, f32[2,256,256]{2,1,0:T(8,128)S(1)} %get-tuple-element.9.probe_ref, ...), custom_call_target="tpu_custom_call" | custom-call | flops 1000000000 | bytes 1048576 | tf_op jit(solution)/shard_map/finish/pallas_call | solution.py:630
  67.1 0.9 %write.1 = (f32[2,128,256]{2,1,0:T(8,128)}, f32[2,256,256]{2,1,0:T(8,128)}) custom-call(f32[2,128,256]{2,1,0:T(8,128)S(1)} %get-tuple-element.12.spec_ref, f32[64,2,8,128]{3,2,1,0:T(8,128)S(1)} %get-tuple-element.13.g_ref), custom_call_target="tpu_custom_call" | custom-call | tf_op jit(solution)/shard_map/write/pallas_call | solution.py:695
Async XLA Ops:
  0.6 15.9 %copy-start.1 = (bf16[2,2,2,256,256]{4,3,2,1,0:T(8,128)(2,1)S(1)}, bf16[2,2,2,256,256]{4,3,2,1,0:T(8,128)(2,1)}, u32[]{:S(2)}) copy-start(bf16[2,2,2,256,256]{4,3,2,1,0:T(8,128)(2,1)} %constant.4.clone.tables) | copy-start | bytes 3145732
  0.6 15.9 %copy-start = (f32[2,128,256]{2,1,0:T(8,128)S(1)}, f32[2,128,256]{2,1,0:T(8,128)}, u32[]{:S(2)}) copy-start(f32[2,128,256]{2,1,0:T(8,128)} %spec_ref.1) | copy-start | bytes 786436
